TPU v7x, 128 devices: a whole 4x4x4 slice. The times are simulated.
128 devices in a mesh: tok: 8 (over z, core), hid: 16 (over x, y).
Axes of the slice: x: 4, y: 4, z: 4, core: 2. Of those that a mesh axis runs over, the one named last changes fastest.
Arguments:
- tokens: bfloat16 [1024, 4096], P('tok', 'hid'), may hold values from -6 to 6
- out_grad: bfloat16 [1024, 4096], P('tok', 'hid'), may hold values from -6 to 6
- routing_ids: int32 [1024, 2], P('tok'), may hold values from 0 to 7, all different within a row; in each aligned block of 128 rows (0 to 127, 128 to 255, ...) at most 48 rows name the same one
- route_weights: bfloat16 [1024, 2], P('tok'), may hold values from 0.049804688 to 1
- gate_matrix: bfloat16 [8, 4096, 8192], P('tok', None, 'hid'), may hold values from -0.125 to 0.125
- up_matrix: bfloat16 [8, 4096, 8192], P('tok', None, 'hid'), may hold values from -0.09375 to 0.09375
- down_matrix: bfloat16 [8, 8192, 4096], P('tok', 'hid'), may hold values from -0.0625 to 0.0625
Outputs:
- input_grad: bfloat16 [1024, 4096], P('tok', 'hid')
- route_grad: bfloat16 [1024, 2], P('tok')
- gate_matrix_grad: bfloat16 [8, 4096, 8192], P('tok', None, 'hid')
- up_matrix_grad: bfloat16 [8, 4096, 8192], P('tok', None, 'hid')
- down_matrix_grad: bfloat16 [8, 8192, 4096], P('tok', 'hid')
Inputs may be any that keep to these rules, and one draw needn't show every extreme that they name: `routing_ids`: each token names two different experts. Among the 128 tokens of one index of tok no expert is named more than 48 times, a bound that some expert reaches in each such block.
All inputs are finite; a program needn't handle non-finite values.
Results may differ from a plain program's by a relative error of at most 0.0076.
Values may be sent and summed in bfloat16 or wider, within the bound.
A program may use at most 128 MiB of HBM per device.

v0:
```python
import math

import jax
import jax.numpy as jnp
from jax import lax
from jax.sharding import PartitionSpec as P


def sent_together(arrays, axis, split_dim, concat_dim, along):
    widths = [math.prod(a.shape[along:]) for a in arrays]
    both = jnp.concatenate(
        [a.reshape(*a.shape[:along], w) for a, w in zip(arrays, widths)], axis=along
    )
    filled = lax.all_to_all(both, axis, split_axis=split_dim, concat_axis=concat_dim, tiled=True)
    tiles = jnp.split(filled, [sum(widths[:k]) for k in range(1, len(widths))], axis=along)
    return tuple(
        (b.reshape(*filled.shape[:along], *a.shape[along:]) for a, b in zip(arrays, tiles))
    )


def in_one_piece(arrays, axis, dim, along):
    both = jnp.concatenate(arrays, axis=along)
    filled, at, done = (lax.all_gather(both, axis, axis=dim, tiled=True), 0, [])
    for a in arrays:
        done.append(lax.slice_in_dim(filled, at, at + a.shape[along], axis=along))
        at += a.shape[along]
    return tuple(done)


def split_up(array, dim, count):
    before, after = (array.shape[:dim], array.shape[dim + 1 :])
    return jnp.moveaxis(array.reshape(*before, count, -1, *after), dim, 0)


def sent_and_summed(array, axis, dim):
    count = lax.axis_size(axis)
    tiles = lax.all_to_all(split_up(array, dim, count), axis, 0, 0, tiled=True)
    return jnp.sum(tiles.astype(jnp.float32), axis=0)


def sent_to_all(array, axis):
    copies = jnp.broadcast_to(array, (lax.axis_size(axis), *array.shape))
    return lax.all_to_all(copies, axis, split_axis=0, concat_axis=0, tiled=True)


def taken_together(array, axis):
    return sent_to_all(array, axis).sum(axis=0)


def contract(left, right, left_dim, right_dim):
    return lax.dot_general(
        left, right, (((left_dim,), (right_dim,)), ((), ())), preferred_element_type=jnp.float32
    )


def per_device(tokens, out_grad, routing_ids, route_weights, gate_matrix, up_matrix, down_matrix):
    groups = lax.axis_size("tok")
    tok_rows = tokens.shape[0]
    capacity = 3 * tok_rows // groups
    flat = routing_ids.reshape(-1)
    choices = flat.shape[0]
    onehot = (flat[:, None] == jnp.arange(groups, dtype=jnp.int32)[None, :]).astype(jnp.int32)
    position = jnp.sum((jnp.cumsum(onehot, axis=0) - onehot) * onehot, axis=1)
    slots = flat * capacity + position
    source = (
        jnp.full((groups * capacity,), choices, jnp.int32)
        .at[slots]
        .set(jnp.arange(choices, dtype=jnp.int32))
    )
    valid = source < choices
    clipped = jnp.minimum(source, choices - 1)
    token_row = clipped // 2
    slot_weight = jnp.where(valid, route_weights.reshape(-1)[clipped], jnp.zeros((), jnp.bfloat16))

    def pack(rows):
        return jnp.where(valid[:, None], rows[token_row], jnp.zeros((), rows.dtype))

    slice_in, slice_grad, rows_weight = sent_together(
        (pack(tokens), pack(out_grad), slot_weight), "tok", 0, 0, 1
    )
    rows_in, rows_grad = in_one_piece((slice_in, slice_grad), "hid", 1, 0)
    gate_w = gate_matrix[0]
    up_w = up_matrix[0]
    down_w = down_matrix[0]
    gate = contract(rows_in, gate_w, 1, 0)
    upper = contract(rows_in, up_w, 1, 0)
    sig = jax.nn.sigmoid(gate)
    act = gate * sig
    weight_col = rows_weight.astype(jnp.float32)[:, None]
    hidden = (act * upper).astype(jnp.bfloat16)
    scaled = (act * upper * weight_col).astype(jnp.bfloat16)
    back = contract(rows_grad, down_w, 1, 1)
    route_local = jnp.sum(hidden.astype(jnp.float32) * back, axis=1)
    back_scaled = back * weight_col
    up_delta = (back_scaled * act).astype(jnp.bfloat16)
    gate_delta = (back_scaled * upper * sig * (1.0 + gate * (1.0 - sig))).astype(jnp.bfloat16)
    gate_out = contract(rows_in, gate_delta, 0, 0).astype(jnp.bfloat16)
    up_out = contract(rows_in, up_delta, 0, 0).astype(jnp.bfloat16)
    down_out = contract(scaled, rows_grad, 0, 0).astype(jnp.bfloat16)
    shares = sent_and_summed(
        (contract(gate_w, gate_delta, 1, 1) + contract(up_w, up_delta, 1, 1)).astype(jnp.bfloat16),
        "hid",
        0,
    )
    route_total = taken_together(route_local, "hid")
    back_rows, back_route = (
        lax.all_to_all(shares.astype(jnp.bfloat16), "tok", split_axis=1, concat_axis=1, tiled=True),
        lax.all_to_all(
            route_total.astype(jnp.bfloat16)[None, :],
            "tok",
            split_axis=1,
            concat_axis=1,
            tiled=True,
        ),
    )
    picked = jnp.take(back_rows, slots, axis=1).astype(jnp.float32)
    features = picked.shape[0]
    input_grad = jnp.sum(picked.reshape(features, tok_rows, 2), axis=2).T.astype(jnp.bfloat16)
    route_grad = jnp.take(back_route[0], slots).reshape(tok_rows, 2)
    return (input_grad, route_grad, gate_out[None], up_out[None], down_out[None])


def solution(mesh):
    in_specs = (
        P("tok", "hid"),
        P("tok", "hid"),
        P("tok", None),
        P("tok", None),
        P("tok", None, "hid"),
        P("tok", None, "hid"),
        P("tok", "hid", None),
    )
    out_specs = (
        P("tok", "hid"),
        P("tok", None),
        P("tok", None, "hid"),
        P("tok", None, "hid"),
        P("tok", "hid", None),
    )
    return jax.shard_map(
        per_device, mesh=mesh, in_specs=in_specs, out_specs=out_specs, check_vma=False
    )
```

profile of v0, /device:TPU:1, one launch (start us, length us, event | category | flops | bytes accessed | tf_op | source)
XLA Modules:
  0.0 210.0 jit_solution(765833599515803562)
XLA Ops:
  7.2 0.0 copy-start
  7.2 0.0 copy-start.1
  7.2 0.0 all-gather.2.cloned.1.call-start
  7.2 0.8 copy.49
  8.0 0.1 eq.26
  8.2 0.1 reshape.122
  8.3 0.6 reduce-window.6
  8.9 0.2 slice_reduce_fusion
  9.2 0.1 mul.70
  9.3 0.1 fusion.23
  9.4 1.4 scatter_custom_fusion
  10.9 0.8 copy.52
  11.6 0.1 reshape.124
  11.8 2.7 %gather_fusion.2 = bf16[384]{0:T(512)(128)(2,1)S(1)} fusion(bf16[256]{0:T(256)(128)(2,1)S(1)} %reshape.124, s32[1024]{0:T(1024)S(1)} %get-tuple-element.48), kind=kCustom, calls=%fused_computation.2 | custom fusion | bytes 3072 | tf_op jit(solution)/shard_map/gather | solution.py:73
  14.5 0.1 broadcast_in_dim.64
  14.6 0.0 copy-done
  14.6 2.1 gather_fusion
  16.7 0.0 copy-done.1
  16.7 2.1 gather_fusion.1
  18.8 0.2 concatenate.12
  19.0 0.1 broadcast_select_fusion.2
  19.2 15.6 %all_to_all.38 = bf16[8,48,513]{2,1,0:T(8,128)(2,1)S(1)} all-to-all(bf16[8,48,513]{2,1,0:T(8,128)(2,1)S(1)} %pad_maximum_fusion), channel_id=1, replica_groups=mesh['tok'=8,'hid'=16] {'tok'}, dimensions={0} | all-to-all | bytes 787968 | tf_op jit(solution)/shard_map/all_to_all | solution.py:14
  34.8 0.8 pad_maximum_fusion.1
  35.6 0.0 all-gather.2.cloned.1.call-update
  35.6 0.1 convert_reduce_fusion
  35.7 65.3 %all-gather.2.cloned.1.call-done = bf16[768,4096]{1,0:T(8,128)(2,1)} async-done(((bf16[768,256]{1,0:T(8,128)(2,1)}), bf16[768,4096]{1,0:T(8,128)(2,1)}) %all-gather.2.cloned.1.call-update) | async-done | bytes 6291472 | tf_op jit(solution)/shard_map/all_gather | solution.py:23
  101.0 5.1 %fusion.5 = f32[384,512]{1,0:T(8,128)S(1)} fusion(bf16[1,4096,512]{2,1,0:T(8,128)(2,1)} %param.11, bf16[768,4096]{1,0:T(8,128)(2,1)} %all-gather.2.cloned.1.call-done), kind=kOutput, calls=%fused_computation.15 | convolution fusion | flops 1610612736 | bytes 8126464 | tf_op jit(solution)/shard_map/dot_general | solution.py:51
  106.0 0.0 copy-done.2
  106.1 1.1 copy-done.6
  107.2 1.8 fusion.8
  109.0 0.0 copy-done.8
  109.0 0.7 copy-done.7
  109.6 2.2 %multiply_reduce_fusion = (f32[384]{0:T(512)S(1)}, bf16[384,512]{1,0:T(8,128)(2,1)S(1)}, bf16[384,512]{1,0:T(8,128)(2,1)S(1)}) fusion(f32[384,512]{1,0:T(8,128)S(1)} %fusion.8, f32[384,512]{1,0:T(8,128)S(1)} %fusion.5, f32[384]{0:T(512)S(1)} %convert_reduce_fusion, bf16[1,512,4096]{2,1,0:T(8,128)(2,1)S(1)} %copy-done.7, bf16[768,4096]{1,0:T(8,128)(2,1)S(1)} %copy-done.6), kind=kOutput, calls=%fused_computation.30 | convolution fusion | flops 1614347904 | bytes 9702912 | tf_op jit(solution)/shard_map/dot_general | solution.py:51
  111.9 0.0 copy-done.10
  111.9 0.0 copy-start.5
  111.9 0.7 broadcast_in_dim.71
  112.6 4.7 %all-to-all-start.3 = ((f32[16,1,384]{2,1,0:T(1,128)}), f32[16,1,384]{2,1,0:T(1,128)S(1)}, u32[]{:S(2)}, u32[]{:S(2)}) async-start(f32[16,1,384]{2,1,0:T(1,128)} %broadcast_in_dim.71), calls=%async_computation.3 | async-start | bytes 49152 | tf_op jit(solution)/shard_map/all_to_all | solution.py:43
  117.3 6.7 %fusion.3 = f32[384,4096]{1,0:T(8,128)} fusion(bf16[384,512]{1,0:T(8,128)(2,1)S(1)} %get-tuple-element.40, bf16[1,4096,512]{2,1,0:T(8,128)(2,1)} %param.11), kind=kOutput, calls=%fused_computation.13 | convolution fusion | flops 1610612736 | bytes 10878976 | tf_op jit(solution)/shard_map/dot_general | solution.py:51
  123.9 0.0 copy-done.5
  123.9 0.0 all-to-all-done.3
  124.0 0.7 convert_element_type.76
  124.7 7.7 %all-to-all-start.4 = ((bf16[1,8,48]{2,0,1:T(2,128)(2,1)}), bf16[1,8,48]{2,0,1:T(2,128)(2,1)S(1)}, u32[]{:S(2)}, u32[]{:S(2)}) async-start(bf16[1,8,48]{2,0,1:T(2,128)(2,1)} %convert_element_type.76), calls=%async_computation.4 | async-start | bytes 8192 | tf_op jit(solution)/shard_map/all_to_all | solution.py:108
  132.3 5.9 %add_convert_fusion = bf16[384,4096]{1,0:T(8,128)(2,1)S(1)} fusion(f32[384,4096]{1,0:T(8,128)} %fusion.3, bf16[384,512]{1,0:T(8,128)(2,1)S(1)} %get-tuple-element.41, bf16[1,4096,512]{2,1,0:T(8,128)(2,1)} %param.12), kind=kOutput, calls=%fused_computation.6 | convolution fusion | flops 1613758464 | bytes 14024704 | tf_op jit(solution)/shard_map/dot_general | solution.py:51
  138.2 2.0 copy.61
  140.3 0.0 all-to-all-done.4
  140.3 6.0 %all-to-all-start.1 = ((bf16[16,256,384]{1,2,0:T(8,128)(2,1)}), bf16[16,256,384]{1,2,0:T(8,128)(2,1)S(1)}, u32[]{:S(2)}, u32[]{:S(2)}) async-start(bf16[16,256,384]{1,2,0:T(8,128)(2,1)} %bitcast.48), calls=%async_computation.1 | async-start | bytes 6291456 | tf_op jit(solution)/shard_map/all_to_all | solution.py:37
  146.3 0.1 reduce_sum.56
  146.4 0.0 slice-start
  146.4 6.5 %fusion = bf16[1,4096,512]{2,1,0:T(8,128)(2,1)} fusion(bf16[384,512]{1,0:T(8,128)(2,1)} %copy-done.5, bf16[768,4096]{1,0:T(8,128)(2,1)} %all-gather.2.cloned.1.call-done), kind=kOutput, calls=%fused_computation.10 | convolution fusion | flops 1612709888 | bytes 7733248 | tf_op jit(solution)/shard_map/dot_general | solution.py:51
  152.9 0.0 copy-done.4
  153.0 6.5 %fusion.1 = bf16[1,4096,512]{2,1,0:T(8,128)(2,1)} fusion(bf16[384,512]{1,0:T(8,128)(2,1)S(1)} %copy-done.4, bf16[768,4096]{1,0:T(8,128)(2,1)} %all-gather.2.cloned.1.call-done), kind=kOutput, calls=%fused_computation.11 | convolution fusion | flops 1612709888 | bytes 7733248 | tf_op jit(solution)/shard_map/dot_general | solution.py:51
  159.4 0.0 slice-done.1
  159.4 4.6 %fusion.2 = bf16[1,512,4096]{2,1,0:T(8,128)(2,1)} fusion(bf16[768,4096]{1,0:T(8,128)(2,1)S(1)} %bitcast.61, f32[384]{0:T(512)S(1)} %convert_reduce_fusion, f32[384,512]{1,0:T(8,128)S(1)} %copy-done.11, f32[384,512]{1,0:T(8,128)S(1)} %copy-done.9), kind=kOutput, calls=%fused_computation.12 | convolution fusion | flops 1614086144 | bytes 8914944 | tf_op jit(solution)/shard_map/dot_general | solution.py:51
  164.0 0.1 squeeze.15
  164.1 1.9 gather_fusion.4
  166.1 0.2 gather.33
  166.2 21.5 %all-to-all-done.1 = bf16[16,256,384]{1,2,0:T(8,128)(2,1)S(1)} async-done(((bf16[16,256,384]{1,2,0:T(8,128)(2,1)}), bf16[16,256,384]{1,2,0:T(8,128)(2,1)S(1)}, u32[]{:S(2)}, u32[]{:S(2)}) %all-to-all-start.1) | async-done | bytes 3145760 | tf_op jit(solution)/shard_map/all_to_all | solution.py:37
  187.7 1.1 reduce_sum.58
  188.8 6.2 %all-to-all-start.2 = ((bf16[256,8,48]{0,2,1:T(8,128)(2,1)}), bf16[256,8,48]{0,2,1:T(8,128)(2,1)S(1)}, u32[]{:S(2)}, u32[]{:S(2)}) async-start(bf16[256,8,48]{0,2,1:T(8,128)(2,1)} %bitcast.11), calls=%async_computation.2 | async-start | bytes 393216 | tf_op jit(solution)/shard_map/all_to_all | solution.py:107
  195.1 0.6 copy.57
  195.7 5.2 %all-to-all-done.2 = bf16[256,8,48]{0,2,1:T(8,128)(2,1)S(1)} async-done(((bf16[256,8,48]{0,2,1:T(8,128)(2,1)}), bf16[256,8,48]{0,2,1:T(8,128)(2,1)S(1)}, u32[]{:S(2)}, u32[]{:S(2)}) %all-to-all-start.2) | async-done | bytes 196640 | tf_op jit(solution)/shard_map/all_to_all | solution.py:107
  200.9 1.2 gather_fusion.3
  202.0 0.1 gather.31
  202.1 1.0 fusion.21
  (30 shorter events, 0.3 us)
Async XLA Ops:
  7.2 7.4 %copy-start = (bf16[128,256]{1,0:T(8,128)(2,1)S(1)}, bf16[128,256]{1,0:T(8,128)(2,1)}, u32[]{:S(2)}) copy-start(bf16[128,256]{1,0:T(8,128)(2,1)} %param.7) | copy-start | bytes 196612
  7.2 9.5 %copy-start.1 = (bf16[128,256]{1,0:T(8,128)(2,1)S(1)}, bf16[128,256]{1,0:T(8,128)(2,1)}, u32[]{:S(2)}) copy-start(bf16[128,256]{1,0:T(8,128)(2,1)} %param.8) | copy-start | bytes 196612
  7.2 93.8 %all-gather.2.cloned.1.call-start = ((), (), s32[]{:S(2)}) async-start(), calls=%async_computation.5 | async-start | bytes 6684672 | tf_op jit(solution)/shard_map/all_gather | solution.py:23
  101.0 5.1 %copy-start.2 = (bf16[1,4096,512]{2,1,0:T(8,128)(2,1)S(1)}, bf16[1,4096,512]{2,1,0:T(8,128)(2,1)}, u32[]{:S(2)}) copy-start(bf16[1,4096,512]{2,1,0:T(8,128)(2,1)} %param.12) | copy-start | bytes 12582916
  101.0 6.2 %copy-start.6 = (bf16[768,4096]{1,0:T(8,128)(2,1)S(1)}, bf16[768,4096]{1,0:T(8,128)(2,1)}, u32[]{:S(2)}) copy-start(bf16[768,4096]{1,0:T(8,128)(2,1)} %all-gather.2.cloned.1.call-done) | copy-start | bytes 18874372
  107.2 1.8 copy-start.8
  107.2 2.5 %copy-start.7 = (bf16[1,512,4096]{2,1,0:T(8,128)(2,1)S(1)}, bf16[1,512,4096]{2,1,0:T(8,128)(2,1)}, u32[]{:S(2)}) copy-start(bf16[1,512,4096]{2,1,0:T(8,128)(2,1)} %param.13) | copy-start | bytes 12582916
  109.6 2.2 %copy-start.10 = (f32[384,512]{1,0:T(8,128)}, f32[384,512]{1,0:T(8,128)S(1)}, u32[]{:S(2)}) copy-start(f32[384,512]{1,0:T(8,128)S(1)} %fusion.8) | copy-start | bytes 2359300
  111.9 12.1 %copy-start.5 = (bf16[384,512]{1,0:T(8,128)(2,1)}, bf16[384,512]{1,0:T(8,128)(2,1)S(1)}, u32[]{:S(2)}) copy-start(bf16[384,512]{1,0:T(8,128)(2,1)S(1)} %get-tuple-element.40) | copy-start | bytes 1179652
  111.9 20.5 %copy-start.3 = (bf16[384,512]{1,0:T(8,128)(2,1)}, bf16[384,512]{1,0:T(8,128)(2,1)S(1)}, u32[]{:S(2)}) copy-start(bf16[384,512]{1,0:T(8,128)(2,1)S(1)} %get-tuple-element.41) | copy-start | bytes 1179652
  112.6 11.3 %all-to-all-start.3 = ((f32[16,1,384]{2,1,0:T(1,128)}), f32[16,1,384]{2,1,0:T(1,128)S(1)}, u32[]{:S(2)}, u32[]{:S(2)}) async-start(f32[16,1,384]{2,1,0:T(1,128)} %broadcast_in_dim.71), calls=%async_computation.3 | async-start | bytes 49152 | tf_op jit(solution)/shard_map/all_to_all | solution.py:43
  124.7 15.6 %all-to-all-start.4 = ((bf16[1,8,48]{2,0,1:T(2,128)(2,1)}), bf16[1,8,48]{2,0,1:T(2,128)(2,1)S(1)}, u32[]{:S(2)}, u32[]{:S(2)}) async-start(bf16[1,8,48]{2,0,1:T(2,128)(2,1)} %convert_element_type.76), calls=%async_computation.4 | async-start | bytes 8192 | tf_op jit(solution)/shard_map/all_to_all | solution.py:108
  140.3 47.4 %all-to-all-start.1 = ((bf16[16,256,384]{1,2,0:T(8,128)(2,1)}), bf16[16,256,384]{1,2,0:T(8,128)(2,1)S(1)}, u32[]{:S(2)}, u32[]{:S(2)}) async-start(bf16[16,256,384]{1,2,0:T(8,128)(2,1)} %bitcast.48), calls=%async_computation.1 | async-start | bytes 6291456 | tf_op jit(solution)/shard_map/all_to_all | solution.py:37
  146.4 6.5 %copy-start.4 = (bf16[384,512]{1,0:T(8,128)(2,1)S(1)}, bf16[384,512]{1,0:T(8,128)(2,1)}, u32[]{:S(2)}) copy-start(bf16[384,512]{1,0:T(8,128)(2,1)} %copy-done.3) | copy-start | bytes 1179652
  146.4 13.0 %slice-start = ((s8[6291456]{0:T(1024)(128)(4,1)}), s8[4194304]{0:T(1024)(128)(4,1)S(1)}, s32[]{:S(2)}) async-start(s8[6291456]{0:T(1024)(128)(4,1)} %bitcast.60), calls=%async_computation.6 | async-start | bytes 8388608
  152.9 6.5 %slice-start.1 = ((s8[6291456]{0:T(1024)(128)(4,1)}), s8[2097152]{0:T(1024)(128)(4,1)S(1)}, s32[]{:S(2)}) async-start(s8[6291456]{0:T(1024)(128)(4,1)} %bitcast.60), calls=%async_computation.7 | async-start | bytes 4194304
  152.9 6.5 %copy-start.9 = (f32[384,512]{1,0:T(8,128)S(1)}, f32[384,512]{1,0:T(8,128)}, u32[]{:S(2)}) copy-start(f32[384,512]{1,0:T(8,128)} %copy-done.8) | copy-start | bytes 2359300
  152.9 6.5 %copy-start.11 = (f32[384,512]{1,0:T(8,128)S(1)}, f32[384,512]{1,0:T(8,128)}, u32[]{:S(2)}) copy-start(f32[384,512]{1,0:T(8,128)} %copy-done.10) | copy-start | bytes 2359300
  188.8 12.1 %all-to-all-start.2 = ((bf16[256,8,48]{0,2,1:T(8,128)(2,1)}), bf16[256,8,48]{0,2,1:T(8,128)(2,1)S(1)}, u32[]{:S(2)}, u32[]{:S(2)}) async-start(bf16[256,8,48]{0,2,1:T(8,128)(2,1)} %bitcast.11), calls=%async_computation.2 | async-start | bytes 393216 | tf_op jit(solution)/shard_map/all_to_all | solution.py:107
Sparse Core Ops, SparseCore 0:
  35.7 65.2 all-gather.1
where the time goes:
time: 213 us; the launch traced here: 210 us
  waiting for transfers between devices  92 us (43%)
  matrix products  39.1 us (18%)
  starting transfers between devices  24.6 us (12%)
  local copies, waits for them, and re-layouts  20.3 us (10%)
  blocking collectives  15.6 us (7%)
  between operations  14.3 us (7%)
  other arithmetic  4.06 us (2%)
    all_gather x1, waiting for transfers between devices, in_one_piece(): filled, at, done = (lax.all_gather(both, axis, axis=dim, tiled=True), 0, [])  65.3 us
    dot_general x8, matrix products, contract(): lax.dot_general(left, right, (((left_dim,), (right_dim,)), ((), ())), pre...  39.1 us
    all_to_all x1, waiting for transfers between devices, sent_and_summed(): tiles = lax.all_to_all(split_up(array, dim, count), axis, 0, 0, tiled=True)  21.5 us
    all_to_all x1, blocking collectives, sent_together(): lax.all_to_all(both, axis, split_axis=split_dim, concat_axis=concat_dim,...  15.6 us
    all_to_all x1, starting transfers between devices, per_device(): lax.all_to_all(route_total.astype(jnp.bfloat16)[None, :], 'tok', split_ax...  7.68 us
    all_to_all x1, starting transfers between devices, per_device(): lax.all_to_all(shares.astype(jnp.bfloat16), 'tok', split_axis=1, concat_a...  6.19 us
    all_to_all x1, starting transfers between devices, sent_and_summed(): tiles = lax.all_to_all(split_up(array, dim, count), axis, 0, 0, tiled=True)  6.01 us
    all_to_all x1, waiting for transfers between devices, per_device(): lax.all_to_all(shares.astype(jnp.bfloat16), 'tok', split_axis=1, concat_a...  5.22 us
  transfers between devices with their start and end apart: 5, of which 3 were waited for; matrix products, arithmetic and copies ran while one was open for 17% of the time, Pallas kernels for 0%

commit v1 on v0

v1 whole, which is shorter than its diff:
```python
import jax
import jax.numpy as jnp
from jax import lax
from jax.experimental import pallas as pl
from jax.experimental.pallas import tpu as pltpu
from jax.sharding import PartitionSpec as P

BF = jnp.bfloat16
F32 = jnp.float32
I32 = jnp.int32
NT = 8
NH = 16
SIGN = (1, -1)


def dot(a, b):
    return lax.dot_general(a, b, (((1,), (0,)), ((), ())), preferred_element_type=F32)


def dot_nt(a, b):
    return lax.dot_general(a, b, (((1,), (1,)), ((), ())), preferred_element_type=F32)


def m4(v):
    return lax.rem(v + 8, 4)


def pick(index, values):
    out = values[-1]
    for k in range(len(values) - 2, -1, -1):
        out = jnp.where(index == k, values[k], out)
    return out


def loop(lo, hi, body):
    def step(i, carry):
        body(i)
        return carry

    lax.fori_loop(lo, hi, step, 0)


def exchange(
    ids_ref, rw_ref, tok_ref, og_ref, wg_hbm, wu_hbm, wd_hbm,
    ig_ref, rg_ref, xt_out, g_out, d_out, hpt_out,
    wg, wu, wd, sel, selt, pack, psend, precv, xg, xt, acc_g, acc_u, acc_r,
    dd, hp, hpt, qs, qr, qt, qb,
    eb, rl1s, rl1r, fn1s, fn1r, rl2s, rl2r, fn2s, fn2r, shr, rb,
    w_sem, o_sem, zs, zr, gs, gr, r1s, r1r, f1s, f1r, r2s, r2r, f2s, f2r,
    qss, qsr, bs, br, cs, cr,
):
    t = lax.axis_index("tok")
    hid = lax.axis_index("hid")
    cx = lax.div(hid, 4)
    cy = lax.rem(hid, 4)
    cap = sel.shape[1]
    rows = NT * cap
    fb = xg.shape[-1]
    hu = wg.shape[-1]

    def to_hid(src, dst, ssem, rsem, target):
        return pltpu.make_async_remote_copy(
            src_ref=src, dst_ref=dst, send_sem=ssem, recv_sem=rsem,
            device_id={"hid": target}, device_id_type=pl.DeviceIdType.MESH,
        )

    def to_tok(src, dst, ssem, rsem, target):
        return pltpu.make_async_remote_copy(
            src_ref=src, dst_ref=dst, send_sem=ssem, recv_sem=rsem,
            device_id={"tok": target}, device_id_type=pl.DeviceIdType.MESH,
        )

    bar = pltpu.get_barrier_semaphore()
    loop(1, NT, lambda k: pl.semaphore_signal(
        bar, inc=1, device_id={"tok": lax.rem(t + k, NT)}, device_id_type=pl.DeviceIdType.MESH))
    loop(1, NH, lambda k: pl.semaphore_signal(
        bar, inc=1, device_id={"hid": lax.rem(hid + k, NH)}, device_id_type=pl.DeviceIdType.MESH))

    w_copies = [
        pltpu.make_async_copy(wg_hbm, wg, w_sem.at[0]),
        pltpu.make_async_copy(wu_hbm, wu, w_sem.at[1]),
        pltpu.make_async_copy(wd_hbm, wd, w_sem.at[2]),
    ]
    for c in w_copies:
        c.start()

    n_tok = tok_ref.shape[0]
    ids = ids_ref[...]
    rw = rw_ref[...].astype(F32)
    expert = lax.broadcasted_iota(I32, (NT, n_tok), 0)
    first = ids[0:1, :] == expert
    second = ids[1:2, :] == expert
    named = jnp.where(first, 1.0, 0.0) + jnp.where(second, 1.0, 0.0)
    weight = jnp.where(first, rw[0:1, :], 0.0) + jnp.where(second, rw[1:2, :], 0.0)
    earlier = (
        lax.broadcasted_iota(I32, (n_tok, n_tok), 0) < lax.broadcasted_iota(I32, (n_tok, n_tok), 1)
    )
    place = dot(named.astype(BF), jnp.where(earlier, 1.0, 0.0).astype(BF))
    code = jnp.where(named > 0.5, place, -1.0).astype(I32)
    slot = lax.broadcasted_iota(I32, (cap, n_tok), 0)
    lane = lax.broadcasted_iota(I32, (cap, n_tok), 1)
    diag = slot == lane
    for e in range(NT):
        one = jnp.where(slot == code[e : e + 1, :], 1.0, 0.0)
        sel[e] = one
        col = jnp.sum(one * weight[e : e + 1, :], axis=1, keepdims=True)
        row = jnp.sum(jnp.where(diag, col, 0.0), axis=0, keepdims=True)
        psend[e] = jnp.broadcast_to(row, (8, n_tok))
    picks = sel[...].reshape(rows, n_tok)
    picks_bf = picks.astype(BF)
    pack[0] = dot(picks_bf, tok_ref[...]).astype(BF).reshape(NT, cap, fb)
    pack[1] = dot(picks_bf, og_ref[...]).astype(BF).reshape(NT, cap, fb)
    xg[0, hid, t] = pack[0, t]
    xg[1, hid, t] = pack[1, t]
    precv[t] = psend[t]

    pl.semaphore_wait(bar, NT - 1 + NH - 1)

    def z_send(a, k):
        to = lax.rem(t + k, NT)
        return to_tok(pack.at[a, to], xg.at[a, hid, t], zs.at[a, k], zr.at[a, k], to)

    def p_send(k):
        to = lax.rem(t + k, NT)
        return to_tok(psend.at[to], precv.at[t], zs.at[2, k], zr.at[2, k], to)

    def z_recv(a, k):
        frm = lax.rem(t + NT - k, NT)
        return to_tok(pack.at[a, frm], xg.at[a, hid, frm], zs.at[a, k], zr.at[a, k], frm)

    def p_recv(k):
        frm = lax.rem(t + NT - k, NT)
        return to_tok(psend.at[frm], precv.at[frm], zs.at[2, k], zr.at[2, k], frm)

    loop(1, NT, lambda k: z_send(0, k).start())
    loop(1, NT, lambda k: z_send(1, k).start())
    loop(1, NT, lambda k: p_send(k).start())

    prim = (cx, cy)
    seco = (cy, cx)

    def blk(a, p, s):
        return 4 * p + s if a == 0 else 4 * s + p

    half = NT // 2

    def gather_copy(a, block, h, sem, target):
        ref = xg.at[a, block] if h is None else xg.at[a, block, pl.ds(h * half, half)]
        return to_hid(ref, ref, gs.at[a, sem], gr.at[a, sem], target)

    def p_own(a, d, recv=False):
        p, s = prim[a], seco[a]
        b = blk(a, m4(p - SIGN[d]) if recv else p, s)
        return gather_copy(a, b, None, d, blk(a, m4(p + SIGN[d]), s))

    def p_fwd(a, d, recv=False):
        p, s = prim[a], seco[a]
        b = blk(a, m4(p - 2 * SIGN[d]) if recv else m4(p - SIGN[d]), s)
        return gather_copy(a, b, d, 2 + d, blk(a, m4(p + SIGN[d]), s))

    def s_own(a, o, d, recv=False):
        p, s = prim[a], seco[a]
        b = blk(a, m4(p + o), m4(s - SIGN[d]) if recv else s)
        return gather_copy(a, b, None, 4 + 2 * o + d, blk(a, p, m4(s + SIGN[d])))

    def s_fwd(a, o, d, recv=False):
        p, s = prim[a], seco[a]
        b = blk(a, m4(p + o), m4(s - 2 * SIGN[d]) if recv else m4(s - SIGN[d]))
        return gather_copy(a, b, d, 12 + 2 * o + d, blk(a, p, m4(s + SIGN[d])))

    for a in range(2):
        loop(1, NT, lambda k: z_recv(a, k).wait_recv())
        for d in range(2):
            p_own(a, d).start()
            s_own(a, 0, d).start()
    loop(1, NT, lambda k: p_recv(k).wait_recv())

    acc_g[...] = jnp.zeros_like(acc_g)
    acc_u[...] = jnp.zeros_like(acc_u)
    acc_r[...] = jnp.zeros_like(acc_r)
    selt[...] = picks.T
    for c in w_copies:
        c.wait()

    o_of = (0, 3, 1, 0, 0, 2, 3, 3, 1, 1, 2, 2, 0, 3, 1, 2)
    q_of = (0, 0, 0, 3, 1, 0, 3, 1, 3, 1, 3, 1, 2, 2, 2, 2)

    def gather_step(j):
        @pl.when(j == 1)
        def _():
            for a in range(2):
                for d in range(2):
                    p_own(a, d, True).wait_recv()
                    p_fwd(a, d).start()
                    for d2 in range(2):
                        s_own(a, (4 - SIGN[d]) % 4, d2).start()
                for d in range(2):
                    s_own(a, 0, d, True).wait_recv()
                    s_fwd(a, 0, d).start()

        @pl.when(j == 5)
        def _():
            for a in range(2):
                for d in range(2):
                    p_fwd(a, d, True).wait_recv()
                for d in range(2):
                    s_own(a, 2, d).start()

        @pl.when(j == 6)
        def _():
            for a in range(2):
                for o in (3, 1):
                    for d in range(2):
                        s_own(a, o, d, True).wait_recv()
                        s_fwd(a, o, d).start()

        @pl.when(j == 10)
        def _():
            for a in range(2):
                for d in range(2):
                    s_own(a, 2, d, True).wait_recv()
                    s_fwd(a, 2, d).start()

        for n, o in ((12, 0), (13, 3), (14, 1), (15, 2)):
            @pl.when(j == n)
            def _():
                for a in range(2):
                    for d in range(2):
                        s_fwd(a, o, d, True).wait_recv()

        o = pick(j, o_of)
        q = pick(j, q_of)
        bx = blk(0, m4(cx + o), m4(cy + q))
        bg = blk(1, m4(cy + o), m4(cx + q))
        x = xg[0, bx].reshape(rows, fb)
        acc_g[...] += dot(x, wg[bx])
        acc_u[...] += dot(x, wu[bx])
        acc_r[...] += dot_nt(xg[1, bg].reshape(rows, fb), wd[:, pl.ds(pl.multiple_of(bg * fb, fb), fb)])
        xt[bx] = x.T

    loop(0, NH, gather_step)

    out_x = pltpu.make_async_copy(xt, xt_out, o_sem.at[0])
    out_g = pltpu.make_async_copy(xg.at[1], g_out, o_sem.at[1])
    out_x.start()
    out_g.start()

    def deltas(b):
        at = pl.ds(pl.multiple_of(b * cap, cap), cap)
        g = acc_g[at, :]
        u = acc_u[at, :]
        r = acc_r[at, :]
        p = jnp.sum(jnp.where(diag, precv[b, 0:1, :], 0.0), axis=1, keepdims=True)
        s = 1.0 / (1.0 + jnp.exp(-g))
        act = g * s
        au = act * u
        hp[at, :] = (au * p).astype(BF)
        q = jnp.sum(au.astype(BF).astype(F32) * r, axis=1, keepdims=True)
        qs[pl.ds(b, 1), :] = jnp.sum(jnp.where(diag, q, 0.0), axis=0, keepdims=True)
        rp = r * p
        dd[at, 0:hu] = (rp * u * s * (1.0 + g * (1.0 - s))).astype(BF)
        dd[at, hu : 2 * hu] = (rp * act).astype(BF)

    loop(0, NT, deltas)

    hrows = rows // 2

    def dprim(a):
        return cx + a * (cy - cx)

    def dseco(a):
        return cy + a * (cx - cy)

    def dblk(a, p, s):
        return (4 * p + s) + a * (3 * s - 3 * p)

    def eblock(a, h):
        at = pl.ds(pl.multiple_of(a * hrows, hrows), hrows)
        return dot_nt(dd[at, 0:hu], wg[h]) + dot_nt(dd[at, hu : 2 * hu], wu[h])

    def rl1(a, d, i):
        return to_hid(rl1s.at[a, d, i], rl1r.at[a, d, i], r1s.at[a, d, i], r1r.at[a, d, i],
                      dblk(a, m4(dprim(a) + 1 - 2 * d), dseco(a)))

    def fn1(a, d, q):
        return to_hid(fn1s.at[a, d, q], fn1r.at[a, d, q], f1s.at[a, d, q], f1r.at[a, d, q],
                      dblk(a, m4(dprim(a) + 1 - 2 * d), dseco(a)))

    def rl2(a, d):
        return to_hid(rl2s.at[a, d], rl2r.at[a, d], r2s.at[a, d], r2r.at[a, d],
                      dblk(a, dprim(a), m4(dseco(a) + 1 - 2 * d)))

    def fn2(a, d):
        return to_hid(fn2s.at[a, d], fn2r.at[a, d], f2s.at[a, d], f2r.at[a, d],
                      dblk(a, dprim(a), m4(dseco(a) + 1 - 2 * d)))

    def relay_step(n):
        a = lax.rem(n, 2)
        d = lax.rem(lax.div(n, 2), 2)
        i = lax.div(n, 4)
        q = 2 - i + d * (1 - 2 * i)
        e = eblock(a, dblk(a, m4(dprim(a) + 2), m4(dseco(a) + q)))
        rl1s[a, d, i] = e.astype(BF)
        rl1(a, d, i).start()

    loop(0, 8, relay_step)

    def q_send(k):
        to = lax.rem(hid + k, NH)
        return to_hid(qs, qr.at[hid], qss.at[k], qsr.at[k], to)

    def q_recv(k):
        frm = lax.rem(hid + NH - k, NH)
        return to_hid(qs, qr.at[frm], qss.at[k], qsr.at[k], frm)

    qr[hid] = qs[...]
    loop(1, NH, lambda k: q_send(k).start())

    q_order = (2, 3, 1, 0)

    def first_step(n):
        a = lax.rem(n, 2)
        d = lax.rem(lax.div(n, 2), 2)
        q = pick(lax.div(n, 4), q_order)
        in_first = jnp.where(d == 0, jnp.where((q == 2) | (q == 1), 1, 0),
                             jnp.where((q == 3) | (q == 0), 1, 0))
        i = jnp.where(d == 0, 2 - q, lax.div(3 - q, 3))
        e = eblock(a, dblk(a, m4(dprim(a) + 1 - 2 * d), m4(dseco(a) + q)))
        eb[...] = e.reshape(2, hrows // 2, fb)

        @pl.when(in_first == 1)
        def _():
            rl1(a, d, i).wait_recv()
            eb[...] += rl1r[a, d, i].astype(F32).reshape(2, hrows // 2, fb)

        fn1s[a, d, q] = eb[...].astype(BF).reshape(hrows, fb)
        fn1(a, d, q).start()

    loop(0, 16, first_step)

    hpt[...] = hp[...].T
    out_h = pltpu.make_async_copy(hpt, hpt_out, o_sem.at[2])
    out_d = pltpu.make_async_copy(dd, d_out, o_sem.at[3])
    out_h.start()
    out_d.start()

    loop(1, NH, lambda k: q_recv(k).wait_recv())
    total = qr[0]
    for h in range(1, NH):
        total = total + qr[h]
    qt[...] = total
    qb[t] = total

    def c_send(k):
        to = lax.rem(t + k, NT)
        return to_tok(qt, qb.at[t], cs.at[k], cr.at[k], to)

    def c_recv(k):
        frm = lax.rem(t + NT - k, NT)
        return to_tok(qt, qb.at[frm], cs.at[k], cr.at[k], frm)

    loop(1, NT, lambda k: c_send(k).start())

    def b_send(b):
        k = lax.rem(b - t + NT, NT)
        return to_tok(shr.at[b], rb.at[t], bs.at[k], br.at[k], b)

    def b_recv(k):
        frm = lax.rem(t + NT - k, NT)
        return to_tok(shr.at[frm], rb.at[frm], bs.at[k], br.at[k], frm)

    def second_step(n):
        a = lax.rem(n, 2)
        q = pick(lax.div(n, 2), q_order)
        e = eblock(a, dblk(a, dprim(a), m4(dseco(a) + q)))
        eb[...] = e.reshape(2, hrows // 2, fb)
        for d in range(2):
            fn1(a, d, q).wait_recv()
        eb[...] += (fn1r[a, 0, q].astype(F32) + fn1r[a, 1, q].astype(F32)).reshape(
            2, hrows // 2, fb)

        @pl.when(q == 2)
        def _():
            for d in range(2):
                rl2s[a, d] = eb[d].astype(BF)
                rl2(a, d).start()

        for d, at in ((0, 1), (1, 3)):
            @pl.when(q == at)
            def _():
                rl2(a, d).wait_recv()
                eb[d] += rl2r[a, d].astype(F32)
                fn2s[a, d] = eb[...].astype(BF)
                fn2(a, d).start()

        @pl.when(q == 0)
        def _():
            for d in range(2):
                fn2(a, d).wait_recv()
            s = eb[...] + fn2r[a, 0].astype(F32) + fn2r[a, 1].astype(F32)
            shr[pl.ds(a * half, half)] = s.astype(BF).reshape(half, cap, fb)
            for i in range(half):
                b = a * half + i

                @pl.when(b != t)
                def _():
                    b_send(b).start()

                @pl.when(b == t)
                def _():
                    rb[t] = shr[t]

    loop(0, 8, second_step)

    loop(1, NT, lambda k: c_recv(k).wait_recv())
    block = lax.broadcasted_iota(I32, (8, n_tok), 0)
    zero = jnp.zeros((1, n_tok), F32)
    route = [zero, zero]
    for e in range(NT):
        row = jnp.sum(jnp.where(block == t, qb[e], 0.0), axis=0, keepdims=True)
        col = jnp.sum(jnp.where(diag, row, 0.0), axis=1, keepdims=True)
        val = jnp.sum(sel[e] * col, axis=0, keepdims=True)
        for k in range(2):
            route[k] = route[k] + jnp.where(ids[k : k + 1, :] == e, val, 0.0)
    rg_ref[...] = jnp.concatenate(route, axis=0).astype(BF)

    loop(1, NT, lambda k: b_recv(k).wait_recv())
    ig_ref[...] = dot(selt[...].astype(BF), rb[...].reshape(rows, fb)).astype(BF)

    def drain_tok(k):
        for a in range(2):
            z_send(a, k).wait_send()
        p_send(k).wait_send()
        c_send(k).wait_send()
        b_send(lax.rem(t + k, NT)).wait_send()

    loop(1, NT, drain_tok)
    loop(1, NH, lambda k: q_send(k).wait_send())
    for a in range(2):
        for d in range(2):
            p_own(a, d).wait_send()
            p_fwd(a, d).wait_send()
            for o in range(4):
                s_own(a, o, d).wait_send()
                s_fwd(a, o, d).wait_send()
            for i in range(2):
                rl1(a, d, i).wait_send()
            for q in range(4):
                fn1(a, d, q).wait_send()
            rl2(a, d).wait_send()
            fn2(a, d).wait_send()
    out_x.wait()
    out_g.wait()
    out_h.wait()
    out_d.wait()


def weight_grads(xt_ref, d_ref, hpt_ref, g_ref, gate_ref, up_ref, down_ref):
    hu = gate_ref.shape[1]
    xt = xt_ref[0]
    gate_ref[...] = dot(xt, d_ref[:, 0:hu]).astype(BF)
    up_ref[...] = dot(xt, d_ref[:, hu : 2 * hu]).astype(BF)
    down_ref[...] = dot(hpt_ref[...], g_ref[0]).astype(BF)


def per_device(tokens, out_grad, routing_ids, route_weights, gate_matrix, up_matrix, down_matrix):
    n_tok, fb = tokens.shape
    cap = 3 * n_tok // NT
    rows = NT * cap
    hu = gate_matrix.shape[2]
    width = gate_matrix.shape[1]
    hr = rows // 2
    vmem = pltpu.VMEM
    dma = pltpu.SemaphoreType.DMA
    any_spec = pl.BlockSpec(memory_space=pl.ANY)
    vm_spec = pl.BlockSpec(memory_space=pltpu.VMEM)
    ig, rg, xt, g, dd, hpt = pl.pallas_call(
        exchange,
        name="exchange",
        out_shape=(
            jax.ShapeDtypeStruct((n_tok, fb), BF),
            jax.ShapeDtypeStruct((2, n_tok), BF),
            jax.ShapeDtypeStruct((NH, fb, rows), BF),
            jax.ShapeDtypeStruct((NH, NT, cap, fb), BF),
            jax.ShapeDtypeStruct((rows, 2 * hu), BF),
            jax.ShapeDtypeStruct((hu, rows), BF),
        ),
        in_specs=[vm_spec] * 4 + [any_spec] * 3,
        out_specs=(vm_spec, vm_spec, any_spec, any_spec, any_spec, any_spec),
        scratch_shapes=[
            vmem((NH, fb, hu), BF), vmem((NH, fb, hu), BF), vmem((hu, width), BF),
            vmem((NT, cap, n_tok), F32), vmem((n_tok, rows), F32),
            vmem((2, NT, cap, fb), BF), vmem((NT, 8, n_tok), F32), vmem((NT, 8, n_tok), F32),
            vmem((2, NH, NT, cap, fb), BF), vmem((NH, fb, rows), BF),
            vmem((rows, hu), F32), vmem((rows, hu), F32), vmem((rows, hu), F32),
            vmem((rows, 2 * hu), BF), vmem((rows, hu), BF), vmem((hu, rows), BF),
            vmem((8, n_tok), F32), vmem((NH, 8, n_tok), F32), vmem((8, n_tok), F32),
            vmem((NT, 8, n_tok), F32),
            vmem((2, hr // 2, fb), F32),
            vmem((2, 2, 2, hr, fb), BF), vmem((2, 2, 2, hr, fb), BF),
            vmem((2, 2, 4, hr, fb), BF), vmem((2, 2, 4, hr, fb), BF),
            vmem((2, 2, hr // 2, fb), BF), vmem((2, 2, hr // 2, fb), BF),
            vmem((2, 2, 2, hr // 2, fb), BF), vmem((2, 2, 2, hr // 2, fb), BF),
            vmem((NT, cap, fb), BF), vmem((NT, cap, fb), BF),
            dma((3,)), dma((4,)),
            dma((3, NT)), dma((3, NT)),
            dma((2, 20)), dma((2, 20)),
            dma((2, 2, 2)), dma((2, 2, 2)),
            dma((2, 2, 4)), dma((2, 2, 4)),
            dma((2, 2)), dma((2, 2)),
            dma((2, 2)), dma((2, 2)),
            dma((NH,)), dma((NH,)),
            dma((NT,)), dma((NT,)),
            dma((NT,)), dma((NT,)),
        ],
        compiler_params=pltpu.CompilerParams(
            collective_id=0, has_side_effects=True, vmem_limit_bytes=52 * 1024 * 1024
        ),
    )(
        routing_ids.T, route_weights.T, tokens, out_grad,
        gate_matrix.reshape(NH, fb, hu), up_matrix.reshape(NH, fb, hu), down_matrix[0],
    )
    gate_out, up_out, down_out = pl.pallas_call(
        weight_grads,
        name="weight_grads",
        grid=(NH,),
        out_shape=(
            jax.ShapeDtypeStruct((width, hu), BF),
            jax.ShapeDtypeStruct((width, hu), BF),
            jax.ShapeDtypeStruct((hu, width), BF),
        ),
        in_specs=[
            pl.BlockSpec((1, fb, rows), lambda i: (i, 0, 0)),
            pl.BlockSpec((rows, 2 * hu), lambda i: (0, 0)),
            pl.BlockSpec((hu, rows), lambda i: (0, 0)),
            pl.BlockSpec((1, rows, fb), lambda i: (i, 0, 0)),
        ],
        out_specs=(
            pl.BlockSpec((fb, hu), lambda i: (i, 0)),
            pl.BlockSpec((fb, hu), lambda i: (i, 0)),
            pl.BlockSpec((hu, fb), lambda i: (0, i)),
        ),
        compiler_params=pltpu.CompilerParams(vmem_limit_bytes=24 * 1024 * 1024),
    )(xt, dd, hpt, g.reshape(NH, rows, fb))
    return (ig, rg.T, gate_out[None], up_out[None], down_out[None])


def solution(mesh):
    in_specs = (
        P("tok", "hid"),
        P("tok", "hid"),
        P("tok", None),
        P("tok", None),
        P("tok", None, "hid"),
        P("tok", None, "hid"),
        P("tok", "hid", None),
    )
    out_specs = (
        P("tok", "hid"),
        P("tok", None),
        P("tok", None, "hid"),
        P("tok", None, "hid"),
        P("tok", "hid", None),
    )
    return jax.shard_map(
        per_device, mesh=mesh, in_specs=in_specs, out_specs=out_specs, check_vma=False
    )
```

time: 213 us -> 102 us (0.48); the launches traced: 210 us -> 101 us
  Pallas kernels: 0 us -> 92.8 us
  waiting for transfers between devices: 92 us -> 0 us
  matrix products: 39.1 us -> 0 us
  starting transfers between devices: 24.6 us -> 0 us
  blocking collectives: 15.6 us -> 0 us
  between operations: 14.3 us -> 0.66 us
  local copies, waits for them, and re-layouts: 20.3 us -> 7.92 us
  other arithmetic: 4.06 us -> 0 us
    pallas_call x0 -> x2, Pallas kernels: none -> 92.8 us  [the longest x1 81.8 us: per_device(): pl.pallas_call(exchange, name='exchange', out_shape=(jax.ShapeDtypeStruct...]
    all_gather x1 -> x0, waiting for transfers between devices: 65.3 us -> none  [in_one_piece(): filled, at, done = (lax.all_gather(both, axis, axis=dim, tiled=True), 0, [])]
    dot_general x8 -> x0, matrix products: 39.1 us -> none  [contract(): lax.dot_general(left, right, (((left_dim,), (right_dim,)), ((), ())), pre...]
    all_to_all x4 -> x0, waiting for transfers between devices: 26.7 us -> none  [the longest x1 21.5 us: sent_and_summed(): tiles = lax.all_to_all(split_up(array, dim, count), axis, 0, 0, tiled=True)]
    all_to_all x4 -> x0, starting transfers between devices: 24.5 us -> none  [the longest x1 7.68 us: per_device(): lax.all_to_all(route_total.astype(jnp.bfloat16)[None, :], 'tok', split_ax...]
    all_to_all x1 -> x0, blocking collectives: 15.6 us -> none  [sent_together(): lax.all_to_all(both, axis, split_axis=split_dim, concat_axis=concat_dim,...]
    gather x7 -> x0, local copies, waits for them, and re-layouts: 10.1 us -> none  [the longest x2 4.11 us: pack(): return jnp.where(valid[:, None], rows[token_row], jnp.zeros((), rows.dtype))]
    unnamed x31 -> x14, local copies, waits for them, and re-layouts: 4.03 us -> 7.92 us
  transfers between devices with their start and end apart: 5 -> 0, of which waited for: 3 -> 0; matrix products, arithmetic and copies ran while one was open for 17% -> 0% of each run, Pallas kernels for 0% -> 0%
where the time goes in v1:
time: 102 us; the launch traced here: 101 us
  Pallas kernels  92.8 us (91%)
  local copies, waits for them, and re-layouts  7.92 us (8%)
    pallas_call x1, Pallas kernels, per_device(): pl.pallas_call(exchange, name='exchange', out_shape=(jax.ShapeDtypeStruct...  81.8 us
    pallas_call x1, Pallas kernels, per_device(): pl.pallas_call(weight_grads, name='weight_grads', grid=(NH,), out_shape=(...  11 us
    unnamed x14, local copies, waits for them, and re-layouts  7.92 us

profile of v1, /device:TPU:1, one launch (start us, length us, event | category | flops | bytes accessed | tf_op | source)
XLA Modules:
  0.0 101.4 jit_solution(10136424700892802214)
XLA Ops:
  0.6 0.0 copy-start.2
  0.6 0.8 copy-done.2
  1.5 0.0 copy-start.3
  1.5 0.8 copy-done.3
  2.3 0.0 copy-start.4
  2.3 0.7 copy-done.4
  3.0 0.0 copy-start.5
  3.0 0.7 copy-done.5
  3.6 81.8 %exchange.1 = (bf16[128,256]{1,0:T(8,128)(2,1)S(1)}, bf16[2,128]{1,0:T(2,128)(2,1)S(1)}, bf16[16,256,384]{2,1,0:T(8,128)(2,1)}, bf16[16,8,48,256]{3,2,1,0:T(8,12...) custom-call(s32[2,128]{1,0:T(2,128)S(1)} %bitcast.11, bf16[2,128]{1,0:T(2,128)(2,1)S(1)} %bitcast.12, ...), custom_call_target="tpu_custom_call" | custom-call | tf_op jit(solution)/shard_map/exchange/pallas_call | solution.py:477
  85.4 0.0 copy-start
  85.4 1.9 %copy-done = bf16[16,256,384]{2,1,0:T(8,128)(2,1)S(1)} copy-done((bf16[16,256,384]{2,1,0:T(8,128)(2,1)S(1)}, bf16[16,256,384]{2,1,0:T(8,128)(2,1)}, u32[]{:S(2)}) %copy-start) | copy-done | bytes 3145752
  87.3 0.0 copy-start.1
  87.3 1.9 %copy-done.1 = bf16[16,8,48,256]{3,2,1,0:T(8,128)(2,1)S(1)} copy-done((bf16[16,8,48,256]{3,2,1,0:T(8,128)(2,1)S(1)}, bf16[16,8,48,256]{3,2,1,0:T(8,128)(2,1)}, u32[]{:S(2)}) %copy-start.1) | copy-done | bytes 3145752
  89.2 11.0 %weight_grads.1 = (bf16[4096,512]{1,0:T(8,128)(2,1)}, bf16[4096,512]{1,0:T(8,128)(2,1)}, bf16[512,4096]{1,0:T(8,128)(2,1)}) custom-call(bf16[16,256,384]{2,1,0:T(8,128)(2,1)S(1)} %copy-done, bf16[384,1024]{1,0:T(8,128)(2,1)S(1)} %get-tuple-element.17.d_ref, bf16[512,384]{1,0:T(8,128)(2,1)S(1)} %get-tuple-element.18.hpt_ref, bf16[16,384,256]{2,1,0:T(8,128)(2,1)S(1)} %bitcast.10), custom_call_target="tpu_custom_call" | custom-call | tf_op jit(solution)/shard_map/weight_grads/pallas_call | solution.py:523
  100.2 0.6 copy.14
  100.9 0.5 copy.15
Async XLA Ops:
  0.6 0.8 copy-start.2
  1.5 0.8 copy-start.3
  2.3 0.7 copy-start.4
  3.0 0.7 copy-start.5
  85.4 1.9 %copy-start = (bf16[16,256,384]{2,1,0:T(8,128)(2,1)S(1)}, bf16[16,256,384]{2,1,0:T(8,128)(2,1)}, u32[]{:S(2)}) copy-start(bf16[16,256,384]{2,1,0:T(8,128)(2,1)} %get-tuple-element.16.xt_ref) | copy-start | bytes 9437188
  87.3 1.9 %copy-start.1 = (bf16[16,8,48,256]{3,2,1,0:T(8,128)(2,1)S(1)}, bf16[16,8,48,256]{3,2,1,0:T(8,128)(2,1)}, u32[]{:S(2)}) copy-start(bf16[16,8,48,256]{3,2,1,0:T(8,128)(2,1)} %get-tuple-element.19) | copy-start | bytes 9437188

commit v2 on v1

--- a/solution.py
+++ b/solution.py
@@ -41,12 +41,12 @@
 
 
 def exchange(
-    ids_ref, rw_ref, tok_ref, og_ref, wg_hbm, wu_hbm, wd_hbm,
-    ig_ref, rg_ref, xt_out, g_out, d_out, hpt_out,
-    wg, wu, wd, sel, selt, pack, psend, precv, xg, xt, acc_g, acc_u, acc_r,
+    ids_hbm, rw_hbm, tok_hbm, og_hbm, wg_hbm, wu_hbm, wd_hbm,
+    ig_ref, rg_ref, gate_ref, up_ref, down_ref,
+    ids_ref, rw_ref, tok_ref, og_ref, wg, wu, wd, sel, selt, pack, psend, precv, xg, xt, acc_g, acc_u, acc_r,
     dd, hp, hpt, qs, qr, qt, qb,
     eb, rl1s, rl1r, fn1s, fn1r, rl2s, rl2r, fn2s, fn2r, shr, rb,
-    w_sem, o_sem, zs, zr, gs, gr, r1s, r1r, f1s, f1r, r2s, r2r, f2s, f2r,
+    w_sem, zs, zr, gs, gr, r1s, r1r, f1s, f1r, r2s, r2r, f2s, f2r,
     qss, qsr, bs, br, cs, cr,
 ):
     t = lax.axis_index("tok")
@@ -70,6 +70,15 @@
             device_id={"tok": target}, device_id_type=pl.DeviceIdType.MESH,
         )
 
+    small = [
+        pltpu.make_async_copy(src, dst, w_sem.at[3 + k])
+        for k, (src, dst) in enumerate(
+            ((ids_hbm, ids_ref), (rw_hbm, rw_ref), (tok_hbm, tok_ref), (og_hbm, og_ref))
+        )
+    ]
+    for c in small:
+        c.start()
+
     bar = pltpu.get_barrier_semaphore()
     loop(1, NT, lambda k: pl.semaphore_signal(
         bar, inc=1, device_id={"tok": lax.rem(t + k, NT)}, device_id_type=pl.DeviceIdType.MESH))
@@ -83,6 +92,9 @@
     ]
     for c in w_copies:
         c.start()
+
+    for c in small:
+        c.wait()
 
     n_tok = tok_ref.shape[0]
     ids = ids_ref[...]
@@ -240,11 +252,6 @@
 
     loop(0, NH, gather_step)
 
-    out_x = pltpu.make_async_copy(xt, xt_out, o_sem.at[0])
-    out_g = pltpu.make_async_copy(xg.at[1], g_out, o_sem.at[1])
-    out_x.start()
-    out_g.start()
-
     def deltas(b):
         at = pl.ds(pl.multiple_of(b * cap, cap), cap)
         g = acc_g[at, :]
@@ -304,6 +311,18 @@
         rl1(a, d, i).start()
 
     loop(0, 8, relay_step)
+    hpt[...] = hp[...].T
+
+    def weight_step(c):
+        at = pl.ds(pl.multiple_of(2 * c * fb, 2 * fb), 2 * fb)
+        x = xt[pl.ds(2 * c, 2)].reshape(2 * fb, rows)
+        gate_ref[at, :] = dot(x, dd[:, 0:hu]).astype(BF)
+        up_ref[at, :] = dot(x, dd[:, hu : 2 * hu]).astype(BF)
+        for i in range(2):
+            h = 2 * c + i
+            down_ref[:, pl.ds(pl.multiple_of(h * fb, fb), fb)] = dot(
+                hpt[...], xg[1, h].reshape(rows, fb)).astype(BF)
+
 
     def q_send(k):
         to = lax.rem(hid + k, NH)
@@ -337,12 +356,7 @@
         fn1(a, d, q).start()
 
     loop(0, 16, first_step)
-
-    hpt[...] = hp[...].T
-    out_h = pltpu.make_async_copy(hpt, hpt_out, o_sem.at[2])
-    out_d = pltpu.make_async_copy(dd, d_out, o_sem.at[3])
-    out_h.start()
-    out_d.start()
+    loop(0, 4, weight_step)
 
     loop(1, NH, lambda k: q_recv(k).wait_recv())
     total = qr[0]
@@ -410,7 +424,12 @@
                 def _():
                     rb[t] = shr[t]
 
-    loop(0, 8, second_step)
+    def second_pair(k):
+        weight_step(4 + k)
+        second_step(2 * k)
+        second_step(2 * k + 1)
+
+    loop(0, 4, second_pair)
 
     loop(1, NT, lambda k: c_recv(k).wait_recv())
     block = lax.broadcasted_iota(I32, (8, n_tok), 0)
@@ -449,18 +468,16 @@
                 fn1(a, d, q).wait_send()
             rl2(a, d).wait_send()
             fn2(a, d).wait_send()
-    out_x.wait()
-    out_g.wait()
-    out_h.wait()
-    out_d.wait()
-
-
-def weight_grads(xt_ref, d_ref, hpt_ref, g_ref, gate_ref, up_ref, down_ref):
-    hu = gate_ref.shape[1]
-    xt = xt_ref[0]
-    gate_ref[...] = dot(xt, d_ref[:, 0:hu]).astype(BF)
-    up_ref[...] = dot(xt, d_ref[:, hu : 2 * hu]).astype(BF)
-    down_ref[...] = dot(hpt_ref[...], g_ref[0]).astype(BF)
+
+
+def copy_out(*refs):
+    n = (len(refs) - 1) // 2
+    sem = refs[2 * n]
+    copies = [pltpu.make_async_copy(refs[k], refs[n + k], sem.at[k]) for k in range(n)]
+    for c in copies:
+        c.start()
+    for c in copies:
+        c.wait()
 
 
 def per_device(tokens, out_grad, routing_ids, route_weights, gate_matrix, up_matrix, down_matrix):
@@ -472,22 +489,23 @@
     hr = rows // 2
     vmem = pltpu.VMEM
     dma = pltpu.SemaphoreType.DMA
-    any_spec = pl.BlockSpec(memory_space=pl.ANY)
+    hbm_spec = pl.BlockSpec(memory_space=pltpu.HBM)
     vm_spec = pl.BlockSpec(memory_space=pltpu.VMEM)
-    ig, rg, xt, g, dd, hpt = pl.pallas_call(
+    shapes = (
+        jax.ShapeDtypeStruct((n_tok, fb), BF),
+        jax.ShapeDtypeStruct((2, n_tok), BF),
+        jax.ShapeDtypeStruct((width, hu), BF),
+        jax.ShapeDtypeStruct((width, hu), BF),
+        jax.ShapeDtypeStruct((hu, width), BF),
+    )
+    held = pl.pallas_call(
         exchange,
         name="exchange",
-        out_shape=(
-            jax.ShapeDtypeStruct((n_tok, fb), BF),
-            jax.ShapeDtypeStruct((2, n_tok), BF),
-            jax.ShapeDtypeStruct((NH, fb, rows), BF),
-            jax.ShapeDtypeStruct((NH, NT, cap, fb), BF),
-            jax.ShapeDtypeStruct((rows, 2 * hu), BF),
-            jax.ShapeDtypeStruct((hu, rows), BF),
-        ),
-        in_specs=[vm_spec] * 4 + [any_spec] * 3,
-        out_specs=(vm_spec, vm_spec, any_spec, any_spec, any_spec, any_spec),
+        out_shape=tuple(vmem(s.shape, s.dtype) for s in shapes),
+        in_specs=[hbm_spec] * 7,
+        out_specs=(vm_spec,) * 5,
         scratch_shapes=[
+            vmem((2, n_tok), I32), vmem((2, n_tok), BF), vmem((n_tok, fb), BF), vmem((n_tok, fb), BF),
             vmem((NH, fb, hu), BF), vmem((NH, fb, hu), BF), vmem((hu, width), BF),
             vmem((NT, cap, n_tok), F32), vmem((n_tok, rows), F32),
             vmem((2, NT, cap, fb), BF), vmem((NT, 8, n_tok), F32), vmem((NT, 8, n_tok), F32),
@@ -502,7 +520,7 @@
             vmem((2, 2, hr // 2, fb), BF), vmem((2, 2, hr // 2, fb), BF),
             vmem((2, 2, 2, hr // 2, fb), BF), vmem((2, 2, 2, hr // 2, fb), BF),
             vmem((NT, cap, fb), BF), vmem((NT, cap, fb), BF),
-            dma((3,)), dma((4,)),
+            dma((7,)),
             dma((3, NT)), dma((3, NT)),
             dma((2, 20)), dma((2, 20)),
             dma((2, 2, 2)), dma((2, 2, 2)),
@@ -514,34 +532,24 @@
             dma((NT,)), dma((NT,)),
         ],
         compiler_params=pltpu.CompilerParams(
-            collective_id=0, has_side_effects=True, vmem_limit_bytes=52 * 1024 * 1024
+            collective_id=0, has_side_effects=True, vmem_limit_bytes=38 * 1024 * 1024
         ),
-    )(
-        routing_ids.T, route_weights.T, tokens, out_grad,
-        gate_matrix.reshape(NH, fb, hu), up_matrix.reshape(NH, fb, hu), down_matrix[0],
-    )
-    gate_out, up_out, down_out = pl.pallas_call(
-        weight_grads,
-        name="weight_grads",
-        grid=(NH,),
-        out_shape=(
-            jax.ShapeDtypeStruct((width, hu), BF),
-            jax.ShapeDtypeStruct((width, hu), BF),
-            jax.ShapeDtypeStruct((hu, width), BF),
-        ),
-        in_specs=[
-            pl.BlockSpec((1, fb, rows), lambda i: (i, 0, 0)),
-            pl.BlockSpec((rows, 2 * hu), lambda i: (0, 0)),
-            pl.BlockSpec((hu, rows), lambda i: (0, 0)),
-            pl.BlockSpec((1, rows, fb), lambda i: (i, 0, 0)),
-        ],
-        out_specs=(
-            pl.BlockSpec((fb, hu), lambda i: (i, 0)),
-            pl.BlockSpec((fb, hu), lambda i: (i, 0)),
-            pl.BlockSpec((hu, fb), lambda i: (0, i)),
-        ),
-        compiler_params=pltpu.CompilerParams(vmem_limit_bytes=24 * 1024 * 1024),
-    )(xt, dd, hpt, g.reshape(NH, rows, fb))
+    )(*[
+        pltpu.with_memory_space_constraint(a, pltpu.HBM)
+        for a in (
+            routing_ids.T, route_weights.T, tokens, out_grad,
+            gate_matrix.reshape(NH, fb, hu), up_matrix.reshape(NH, fb, hu), down_matrix[0],
+        )
+    ])
+    ig, rg, gate_out, up_out, down_out = pl.pallas_call(
+        copy_out,
+        name="copy_out",
+        out_shape=shapes,
+        in_specs=[vm_spec] * 5,
+        out_specs=(hbm_spec,) * 5,
+        scratch_shapes=[dma((5,))],
+        compiler_params=pltpu.CompilerParams(vmem_limit_bytes=1024 * 1024),
+    )(*[pltpu.with_memory_space_constraint(a, pltpu.VMEM) for a in held])
     return (ig, rg.T, gate_out[None], up_out[None], down_out[None])
 
 

time: 102 us -> 90.7 us (0.89)
  local copies, waits for them, and re-layouts: 7.92 us -> 0 us
  Pallas kernels: 92.8 us -> 90 us
    unnamed x14 -> x0, local copies, waits for them, and re-layouts: 7.92 us -> none
    pallas_call x2, Pallas kernels: 92.8 us -> 90 us  [the longest x1 85.2 us: per_device(): pl.pallas_call(exchange, name='exchange', out_shape=tuple((vmem(s.shape,...]
where the time goes in v2:
time: 90.7 us; the launch traced here: 90.6 us
  Pallas kernels  90 us (99%)
    pallas_call x1, Pallas kernels, per_device(): pl.pallas_call(exchange, name='exchange', out_shape=tuple((vmem(s.shape,...  85.2 us
    pallas_call x1, Pallas kernels, per_device(): pl.pallas_call(copy_out, name='copy_out', out_shape=shapes, in_specs=[vm_...  4.73 us

profile of v2, /device:TPU:1, one launch (start us, length us, event | category | flops | bytes accessed | tf_op | source)
XLA Modules:
  0.0 90.6 jit_solution(586093618310112377)
XLA Ops:
  0.6 85.2 %exchange.1 = (bf16[128,256]{1,0:T(8,128)(2,1)S(1)}, bf16[2,128]{1,0:T(2,128)(2,1)S(1)}, bf16[4096,512]{1,0:T(8,128)(2,1)S(1)}, bf16[4096,512]{1,0:T(8,128)(2,1)S(1)}, bf16[512,4096]{1,0:T(8,128)(2,1)S(1)}) custom-call(s32[2,128]{1,0:T(2,128)} %bitcast.12, bf16[2,128]{1,0:T(2,128)(2,1)} %bitcast.13, bf16[128,256]{1,0:T(8,128)(2,1)} %tok_hbm.1, ...), custom_call_target="tpu_custom_call" | custom-call | tf_op jit(solution)/shard_map/exchange/pallas_call | solution.py:501
  85.9 4.7 %copy_out.1 = (bf16[128,256]{1,0:T(8,128)(2,1)}, bf16[2,128]{1,0:T(2,128)(2,1)}, bf16[4096,512]{1,0:T(8,128)(2,1)}, bf16[4096,512]{1,0:T(8,128)(2,1)}, bf16[512,4096]{1,0:T(8,128)(2,1)}) custom-call(bf16[128,256]{1,0:T(8,128)(2,1)S(1)} %get-tuple-element.15.refs_0_, bf16[2,128]{1,0:T(2,128)(2,1)S(1)} %get-tuple-element.16.refs_1_, ...), custom_call_target="tpu_custom_call" | custom-call | tf_op jit(solution)/shard_map/copy_out/pallas_call | solution.py:544

commit v3 on v2

v3 whole, which is shorter than its diff:
```python
import jax
import jax.numpy as jnp
from jax import lax
from jax.experimental import pallas as pl
from jax.experimental.pallas import tpu as pltpu
from jax.sharding import PartitionSpec as P

BF = jnp.bfloat16
F32 = jnp.float32
I32 = jnp.int32
NT = 8
NH = 16
SIGN = (1, -1)
PARTNERS = ((0, 1), (2, 0), (2, 1), (1, 0), (1, 1), (3, 0), (3, 1))


def dot(a, b):
    return lax.dot_general(a, b, (((1,), (0,)), ((), ())), preferred_element_type=F32)


def dot_nt(a, b):
    return lax.dot_general(a, b, (((1,), (1,)), ((), ())), preferred_element_type=F32)


def m4(v):
    return lax.rem(v + 8, 4)


def pick(index, values):
    out = values[-1]
    for k in range(len(values) - 2, -1, -1):
        out = jnp.where(index == k, values[k], out)
    return out


def loop(lo, hi, body):
    def step(i, carry):
        body(i)
        return carry

    lax.fori_loop(lo, hi, step, 0)


def exchange(
    ids_hbm, rw_hbm, tok_hbm, og_hbm, wg_hbm, wu_hbm, wd_hbm,
    ig_ref, rg_ref, gate_ref, up_ref, down_ref,
    ids_ref, rw_ref, tok_ref, og_ref, wg, wu, wd, sel, selt, pack, psend, precv, xg, xt, acc_g, acc_u, acc_r,
    dd, hp, hpt, qs, q1, q2, qt, qb,
    e32, rl1s, rl1r, fn1s, fn1r, rl2s, rl2r, fn2s, fn2r, shr, rb,
    w_sem, zs, zr, gs, gr, r1s, r1r, f1s, f1r, r2s, r2r, f2s, f2r,
    qss, qsr, bs, br, cs, cr,
):
    t = lax.axis_index("tok")
    hid = lax.axis_index("hid")
    z = lax.div(t, 2)
    core = lax.rem(t, 2)
    cx = lax.div(hid, 4)
    cy = lax.rem(hid, 4)
    cap = sel.shape[1]
    rows = NT * cap
    fb = xg.shape[-1]
    hu = wg.shape[-1]

    def to_hid(src, dst, ssem, rsem, target):
        return pltpu.make_async_remote_copy(
            src_ref=src, dst_ref=dst, send_sem=ssem, recv_sem=rsem,
            device_id={"hid": target}, device_id_type=pl.DeviceIdType.MESH,
        )

    def to_tok(src, dst, ssem, rsem, target):
        return pltpu.make_async_remote_copy(
            src_ref=src, dst_ref=dst, send_sem=ssem, recv_sem=rsem,
            device_id={"tok": target}, device_id_type=pl.DeviceIdType.MESH,
        )

    small = [
        pltpu.make_async_copy(src, dst, w_sem.at[3 + k])
        for k, (src, dst) in enumerate(
            ((ids_hbm, ids_ref), (rw_hbm, rw_ref), (tok_hbm, tok_ref), (og_hbm, og_ref))
        )
    ]
    for c in small:
        c.start()

    bar = pltpu.get_barrier_semaphore()
    for dz, dc in PARTNERS:
        pl.semaphore_signal(
            bar, inc=1, device_id={"tok": 2 * m4(z + dz) + lax.rem(core + dc, 2)},
            device_id_type=pl.DeviceIdType.MESH)
    for k in range(1, 4):
        for target in (4 * m4(cx + k) + cy, 4 * cx + m4(cy + k)):
            pl.semaphore_signal(
                bar, inc=1, device_id={"hid": target}, device_id_type=pl.DeviceIdType.MESH)

    w_copies = [
        pltpu.make_async_copy(wg_hbm, wg, w_sem.at[0]),
        pltpu.make_async_copy(wu_hbm, wu, w_sem.at[1]),
        pltpu.make_async_copy(wd_hbm, wd, w_sem.at[2]),
    ]
    for c in w_copies:
        c.start()

    for c in small:
        c.wait()

    n_tok = tok_ref.shape[0]
    ids = ids_ref[...]
    rw = rw_ref[...].astype(F32)
    expert = lax.broadcasted_iota(I32, (NT, n_tok), 0)
    first = ids[0:1, :] == expert
    second = ids[1:2, :] == expert
    named = jnp.where(first, 1.0, 0.0) + jnp.where(second, 1.0, 0.0)
    weight = jnp.where(first, rw[0:1, :], 0.0) + jnp.where(second, rw[1:2, :], 0.0)
    earlier = (
        lax.broadcasted_iota(I32, (n_tok, n_tok), 0) < lax.broadcasted_iota(I32, (n_tok, n_tok), 1)
    )
    place = dot(named.astype(BF), jnp.where(earlier, 1.0, 0.0).astype(BF))
    code = jnp.where(named > 0.5, place, -1.0).astype(I32)
    slot = lax.broadcasted_iota(I32, (cap, n_tok), 0)
    lane = lax.broadcasted_iota(I32, (cap, n_tok), 1)
    diag = slot == lane
    for e in range(NT):
        one = jnp.where(slot == code[e : e + 1, :], 1.0, 0.0)
        sel[e] = one
        col = jnp.sum(one * weight[e : e + 1, :], axis=1, keepdims=True)
        row = jnp.sum(jnp.where(diag, col, 0.0), axis=0, keepdims=True)
        psend[e] = jnp.broadcast_to(row, (8, n_tok))
    picks = sel[...].reshape(rows, n_tok)
    picks_bf = picks.astype(BF)
    pack[0] = dot(picks_bf, tok_ref[...]).astype(BF).reshape(NT, cap, fb)
    pack[1] = dot(picks_bf, og_ref[...]).astype(BF).reshape(NT, cap, fb)
    xg[0, hid, core] = pack[0, t]
    xg[1, hid, core] = pack[1, t]
    precv[core] = psend[t]

    pl.semaphore_wait(bar, len(PARTNERS) + 6)

    def partner(m, back):
        dz, dc = PARTNERS[m]
        return 2 * m4(z - dz if back else z + dz) + lax.rem(core + dc, 2)

    def z_send(a, m):
        to = partner(m, False)
        place = 2 * ((4 - PARTNERS[m][0]) % 4) + core
        if a == 2:
            return to_tok(psend.at[to], precv.at[place], zs.at[2, m], zr.at[2, m], to)
        return to_tok(pack.at[a, to], xg.at[a, hid, place], zs.at[a, m], zr.at[a, m], to)

    def z_recv(a, m):
        frm = partner(m, True)
        place = 2 * ((4 - PARTNERS[m][0]) % 4) + lax.rem(core + PARTNERS[m][1], 2)
        if a == 2:
            return to_tok(psend.at[frm], precv.at[place], zs.at[2, m], zr.at[2, m], frm)
        return to_tok(pack.at[a, frm], xg.at[a, hid, place], zs.at[a, m], zr.at[a, m], frm)

    z_send(0, 0).start()
    z_send(1, 0).start()
    for a in range(3):
        for m in range(7):
            if a == 2 or m > 0:
                z_send(a, m).start()

    prim = (cx, cy)
    seco = (cy, cx)

    def blk(a, p, s):
        return 4 * p + s if a == 0 else 4 * s + p

    half = NT // 2
    span = {(0, None): (0, 2), (0, 0): (0, 1), (0, 1): (1, 1),
            (1, None): (2, 6), (1, 0): (2, 3), (1, 1): (5, 3)}

    def gather_copy(a, w, block, h, sem, target):
        first, count = span[w, h]
        ref = xg.at[a, block, pl.ds(first, count)]
        return to_hid(ref, ref, gs.at[w, a, sem], gr.at[w, a, sem], target)

    def p_own(a, w, d, recv=False):
        p, s = prim[a], seco[a]
        b = blk(a, m4(p - SIGN[d]) if recv else p, s)
        return gather_copy(a, w, b, None, d, blk(a, m4(p + SIGN[d]), s))

    def p_fwd(a, w, d, recv=False):
        p, s = prim[a], seco[a]
        b = blk(a, m4(p - 2 * SIGN[d]) if recv else m4(p - SIGN[d]), s)
        return gather_copy(a, w, b, d, 2 + d, blk(a, m4(p + SIGN[d]), s))

    def s_own(a, w, o, d, recv=False):
        p, s = prim[a], seco[a]
        b = blk(a, m4(p + o), m4(s - SIGN[d]) if recv else s)
        return gather_copy(a, w, b, None, 4 + 2 * o + d, blk(a, p, m4(s + SIGN[d])))

    def s_fwd(a, w, o, d, recv=False):
        p, s = prim[a], seco[a]
        b = blk(a, m4(p + o), m4(s - 2 * SIGN[d]) if recv else m4(s - SIGN[d]))
        return gather_copy(a, w, b, d, 12 + 2 * o + d, blk(a, p, m4(s + SIGN[d])))

    def gather_begin(w, a):
        for d in range(2):
            p_own(a, w, d).start()
            s_own(a, w, 0, d).start()

    def gather_1(w, a):
        for d in range(2):
            p_own(a, w, d, True).wait_recv()
            p_fwd(a, w, d).start()
            for d2 in range(2):
                s_own(a, w, (4 - SIGN[d]) % 4, d2).start()
        for d in range(2):
            s_own(a, w, 0, d, True).wait_recv()
            s_fwd(a, w, 0, d).start()

    def gather_5(w, a):
        for d in range(2):
            p_fwd(a, w, d, True).wait_recv()
        for d in range(2):
            s_own(a, w, 2, d).start()

    def gather_pass(w, a, o):
        for d in range(2):
            s_own(a, w, o, d, True).wait_recv()
            s_fwd(a, w, o, d).start()

    for a in range(2):
        z_recv(a, 0).wait_recv()
        gather_begin(0, a)
    acc_g[...] = jnp.zeros_like(acc_g)
    acc_u[...] = jnp.zeros_like(acc_u)
    acc_r[...] = jnp.zeros_like(acc_r)
    selt[...] = picks.T
    for a in range(2):
        gather_1(0, a)
    for a in range(2):
        gather_5(0, a)
    for a in range(2):
        for m in range(1, 7):
            z_recv(a, m).wait_recv()
        gather_begin(1, a)
    for a in range(2):
        for o in (3, 1):
            gather_pass(0, a, o)
    for a in range(2):
        gather_pass(0, a, 2)
    for m in range(7):
        z_recv(2, m).wait_recv()
    for c in w_copies:
        c.wait()

    o_of = (0, 3, 1, 0, 0, 2, 3, 3, 1, 1, 2, 2, 0, 3, 1, 2)
    q_of = (0, 0, 0, 3, 1, 0, 3, 1, 3, 1, 3, 1, 2, 2, 2, 2)

    def gather_step(j):
        @pl.when(j == 1)
        def _():
            for a in range(2):
                gather_1(1, a)

        @pl.when(j == 5)
        def _():
            for a in range(2):
                gather_5(1, a)

        @pl.when(j == 6)
        def _():
            for a in range(2):
                for o in (3, 1):
                    gather_pass(1, a, o)

        @pl.when(j == 10)
        def _():
            for a in range(2):
                gather_pass(1, a, 2)

        for n, o in ((12, 0), (13, 3), (14, 1), (15, 2)):
            @pl.when(j == n)
            def _():
                for a in range(2):
                    for w in range(2):
                        for d in range(2):
                            s_fwd(a, w, o, d, True).wait_recv()

        o = pick(j, o_of)
        q = pick(j, q_of)
        bx = blk(0, m4(cx + o), m4(cy + q))
        bg = blk(1, m4(cy + o), m4(cx + q))
        x = xg[0, bx].reshape(rows, fb)
        acc_g[...] += dot(x, wg[bx])
        acc_u[...] += dot(x, wu[bx])
        acc_r[...] += dot_nt(xg[1, bg].reshape(rows, fb), wd[:, pl.ds(pl.multiple_of(bg * fb, fb), fb)])
        xt[bx] = x.T

    loop(0, NH, gather_step)

    def deltas(b):
        at = pl.ds(pl.multiple_of(b * cap, cap), cap)
        g = acc_g[at, :]
        u = acc_u[at, :]
        r = acc_r[at, :]
        p = jnp.sum(jnp.where(diag, precv[b, 0:1, :], 0.0), axis=1, keepdims=True)
        s = 1.0 / (1.0 + jnp.exp(-g))
        act = g * s
        au = act * u
        hp[at, :] = (au * p).astype(BF)
        q = jnp.sum(au.astype(BF).astype(F32) * r, axis=1, keepdims=True)
        qs[pl.ds(b, 1), :] = jnp.sum(jnp.where(diag, q, 0.0), axis=0, keepdims=True)
        rp = r * p
        dd[at, 0:hu] = (rp * u * s * (1.0 + g * (1.0 - s))).astype(BF)
        dd[at, hu : 2 * hu] = (rp * act).astype(BF)

    loop(0, NT, deltas)

    hrows = rows // 2

    def along(a, d):
        p, s = prim[a], seco[a]
        return blk(a, m4(p + SIGN[d]), s)

    def across(a, d):
        p, s = prim[a], seco[a]
        return blk(a, p, m4(s + SIGN[d]))

    def rl1(a, d, i):
        return to_hid(rl1s.at[a, d, i], rl1r.at[a, d, i], r1s.at[a, d, i], r1r.at[a, d, i], along(a, d))

    def fn1(a, d, q):
        return to_hid(fn1s.at[a, d, q], fn1r.at[a, d, q], f1s.at[a, d, q], f1r.at[a, d, q], along(a, d))

    def rl2(a, d):
        return to_hid(rl2s.at[a, d], rl2r.at[a, d], r2s.at[a, d], r2r.at[a, d], across(a, d))

    def fn2(a, d):
        return to_hid(fn2s.at[a, d], fn2r.at[a, d], f2s.at[a, d], f2r.at[a, d], across(a, d))

    def q_x(k, recv=False):
        frm = m4(cx - k) if recv else cx
        return to_hid(qs, q1.at[frm], qss.at[0, k], qsr.at[0, k], 4 * m4(cx + k) + cy)

    def q_y(k, recv=False):
        frm = m4(cy - k) if recv else cy
        return to_hid(qt, q2.at[frm], qss.at[1, k], qsr.at[1, k], 4 * cx + m4(cy + k))

    x_of = (2, 2, 3, 2, 1, 2, 0, 1, 3, 3, 1, 1, 3, 0, 0, 0)
    y_of = (2, 3, 2, 1, 2, 0, 2, 3, 3, 1, 1, 0, 0, 1, 3, 0)

    def e_step(n):
        h = 4 * m4(cx + pick(n, x_of)) + m4(cy + pick(n, y_of))
        e = dot_nt(dd[:, 0:hu], wg[h]) + dot_nt(dd[:, hu : 2 * hu], wu[h])
        e32[h] = e.reshape(2, hrows, fb)
        for k, (d, i) in ((0, (0, 0)), (1, (1, 0)), (3, (0, 1)), (5, (1, 1))):
            for a in range(2):
                @pl.when(n == (k + a if k else 0))
                def _():
                    rl1s[a, d, i] = e32[h, a].astype(BF)
                    rl1(a, d, i).start()

    loop(0, NH, e_step)

    q1[cx] = qs[...]
    for k in range(1, 4):
        q_x(k).start()

    relayed = {2: (0, 0), 1: (0, 1), 3: (1, 0), 0: (1, 1)}

    def first_step(q):
        way, i = relayed[q]
        for d in (1 - way, way):
            for a in range(2):
                e = e32[blk(a, m4(prim[a] + SIGN[d]), m4(seco[a] + q)), a]
                if d == way:
                    rl1(a, d, i).wait_recv()
                    e = e + rl1r[a, d, i].astype(F32)
                fn1s[a, d, q] = e.astype(BF)
                fn1(a, d, q).start()

    def total_of(a, q):
        for d in range(2):
            fn1(a, d, q).wait_recv()
        return (e32[blk(a, prim[a], m4(seco[a] + q)), a]
                + fn1r[a, 0, q].astype(F32) + fn1r[a, 1, q].astype(F32))

    hpt[...] = hp[...].T

    def weight_step(c):
        at = pl.ds(pl.multiple_of(2 * c * fb, 2 * fb), 2 * fb)
        x = xt[pl.ds(2 * c, 2)].reshape(2 * fb, rows)
        gate_ref[at, :] = dot(x, dd[:, 0:hu]).astype(BF)
        up_ref[at, :] = dot(x, dd[:, hu : 2 * hu]).astype(BF)
        for i in range(2):
            h = 2 * c + i
            down_ref[:, pl.ds(pl.multiple_of(h * fb, fb), fb)] = dot(
                hpt[...], xg[1, h].reshape(rows, fb)).astype(BF)

    first_step(2)
    first_step(3)
    for k in range(1, 4):
        q_x(k, True).wait_recv()
    qt[...] = q1[0] + q1[1] + q1[2] + q1[3]
    q2[cy] = qt[...]
    for k in range(1, 4):
        q_y(k).start()
    loop(0, 2, weight_step)
    first_step(1)
    loop(2, 3, weight_step)
    quarter = hrows // 2
    for a in range(2):
        s = total_of(a, 2)
        for d in range(2):
            rl2s[a, d] = s[d * quarter : (d + 1) * quarter].astype(BF)
            rl2(a, d).start()
    first_step(0)
    loop(3, 6, weight_step)
    for k in range(1, 4):
        q_y(k, True).wait_recv()
    qw = q2[0] + q2[1] + q2[2] + q2[3]
    qsum = qb.at[NT]
    qsum[...] = qw
    qb[t] = qw

    def c_send(m):
        to = partner(m, False)
        return to_tok(qb.at[NT], qb.at[t], cs.at[m], cr.at[m], to)

    def c_recv(m):
        frm = partner(m, True)
        return to_tok(qb.at[NT], qb.at[frm], cs.at[m], cr.at[m], frm)

    for m in range(7):
        c_send(m).start()

    for d, q in ((1, 3), (0, 1)):
        for a in range(2):
            s = total_of(a, q)
            rl2(a, d).wait_recv()
            r = rl2r[a, d].astype(F32)
            at = slice(d * quarter, (d + 1) * quarter)
            other = slice((1 - d) * quarter, (2 - d) * quarter)
            fn2s[a, d, d] = (s[at] + r).astype(BF)
            fn2s[a, d, 1 - d] = s[other].astype(BF)
            fn2(a, d).start()
    loop(6, 8, weight_step)

    def b_send(m):
        to = partner(m, False)
        dz, dc = PARTNERS[m]
        return to_tok(shr.at[2 * dz + lax.rem(core + dc, 2)], rb.at[t], bs.at[m], br.at[m], to)

    def b_recv(m):
        frm = partner(m, True)
        return to_tok(shr.at[0], rb.at[frm], bs.at[m], br.at[m], frm)

    for a in (1, 0):
        s = total_of(a, 0)
        for d in range(2):
            fn2(a, d).wait_recv()
            s = s + fn2r[a, d].astype(F32).reshape(hrows, fb)
        shr[a * half : (a + 1) * half] = s.astype(BF).reshape(half, cap, fb)
        for m, (dz, dc) in enumerate(PARTNERS):
            if dz // 2 == a:
                b_send(m).start()
    rb[t] = shr[core]

    for m in range(7):
        c_recv(m).wait_recv()
    block = lax.broadcasted_iota(I32, (8, n_tok), 0)
    zero = jnp.zeros((1, n_tok), F32)
    route = [zero, zero]
    for e in range(NT):
        row = jnp.sum(jnp.where(block == 2 * m4(z - e // 2) + core, qb[e], 0.0), axis=0, keepdims=True)
        col = jnp.sum(jnp.where(diag, row, 0.0), axis=1, keepdims=True)
        val = jnp.sum(sel[e] * col, axis=0, keepdims=True)
        for k in range(2):
            route[k] = route[k] + jnp.where(ids[k : k + 1, :] == e, val, 0.0)
    rg_ref[...] = jnp.concatenate(route, axis=0).astype(BF)

    for m in range(7):
        b_recv(m).wait_recv()
    ig_ref[...] = dot(selt[...].astype(BF), rb[...].reshape(rows, fb)).astype(BF)

    for m in range(7):
        for a in range(3):
            z_send(a, m).wait_send()
        c_send(m).wait_send()
        b_send(m).wait_send()
    for k in range(1, 4):
        q_x(k).wait_send()
        q_y(k).wait_send()
    for a in range(2):
        for d in range(2):
            for w in range(2):
                p_own(a, w, d).wait_send()
                p_fwd(a, w, d).wait_send()
                for o in range(4):
                    s_own(a, w, o, d).wait_send()
                    s_fwd(a, w, o, d).wait_send()
            for i in range(2):
                rl1(a, d, i).wait_send()
            for q in range(4):
                fn1(a, d, q).wait_send()
            rl2(a, d).wait_send()
            fn2(a, d).wait_send()


def copy_out(*refs):
    n = (len(refs) - 1) // 2
    sem = refs[2 * n]
    copies = [pltpu.make_async_copy(refs[k], refs[n + k], sem.at[k]) for k in range(n)]
    for c in copies:
        c.start()
    for c in copies:
        c.wait()


def per_device(tokens, out_grad, routing_ids, route_weights, gate_matrix, up_matrix, down_matrix):
    n_tok, fb = tokens.shape
    cap = 3 * n_tok // NT
    rows = NT * cap
    hu = gate_matrix.shape[2]
    width = gate_matrix.shape[1]
    hr = rows // 2
    vmem = pltpu.VMEM
    dma = pltpu.SemaphoreType.DMA
    hbm_spec = pl.BlockSpec(memory_space=pltpu.HBM)
    vm_spec = pl.BlockSpec(memory_space=pltpu.VMEM)
    shapes = (
        jax.ShapeDtypeStruct((n_tok, fb), BF),
        jax.ShapeDtypeStruct((2, n_tok), BF),
        jax.ShapeDtypeStruct((width, hu), BF),
        jax.ShapeDtypeStruct((width, hu), BF),
        jax.ShapeDtypeStruct((hu, width), BF),
    )
    held = pl.pallas_call(
        exchange,
        name="exchange",
        out_shape=tuple(vmem(s.shape, s.dtype) for s in shapes),
        in_specs=[hbm_spec] * 7,
        out_specs=(vm_spec,) * 5,
        scratch_shapes=[
            vmem((2, n_tok), I32), vmem((2, n_tok), BF), vmem((n_tok, fb), BF), vmem((n_tok, fb), BF),
            vmem((NH, fb, hu), BF), vmem((NH, fb, hu), BF), vmem((hu, width), BF),
            vmem((NT, cap, n_tok), F32), vmem((n_tok, rows), F32),
            vmem((2, NT, cap, fb), BF), vmem((NT, 8, n_tok), F32), vmem((NT, 8, n_tok), F32),
            vmem((2, NH, NT, cap, fb), BF), vmem((NH, fb, rows), BF),
            vmem((rows, hu), F32), vmem((rows, hu), F32), vmem((rows, hu), F32),
            vmem((rows, 2 * hu), BF), vmem((rows, hu), BF), vmem((hu, rows), BF),
            vmem((8, n_tok), F32), vmem((4, 8, n_tok), F32), vmem((4, 8, n_tok), F32),
            vmem((8, n_tok), F32), vmem((NT + 1, 8, n_tok), F32),
            vmem((NH, 2, hr, fb), F32),
            vmem((2, 2, 2, hr, fb), BF), vmem((2, 2, 2, hr, fb), BF),
            vmem((2, 2, 4, hr, fb), BF), vmem((2, 2, 4, hr, fb), BF),
            vmem((2, 2, hr // 2, fb), BF), vmem((2, 2, hr // 2, fb), BF),
            vmem((2, 2, 2, hr // 2, fb), BF), vmem((2, 2, 2, hr // 2, fb), BF),
            vmem((NT, cap, fb), BF), vmem((NT, cap, fb), BF),
            dma((7,)),
            dma((3, NT)), dma((3, NT)),
            dma((2, 2, 20)), dma((2, 2, 20)),
            dma((2, 2, 2)), dma((2, 2, 2)),
            dma((2, 2, 4)), dma((2, 2, 4)),
            dma((2, 2)), dma((2, 2)),
            dma((2, 2)), dma((2, 2)),
            dma((2, 4)), dma((2, 4)),
            dma((NT,)), dma((NT,)),
            dma((NT,)), dma((NT,)),
        ],
        compiler_params=pltpu.CompilerParams(
            collective_id=0, has_side_effects=True, vmem_limit_bytes=46 * 1024 * 1024
        ),
    )(*[
        pltpu.with_memory_space_constraint(a, pltpu.HBM)
        for a in (
            routing_ids.T, route_weights.T, tokens, out_grad,
            gate_matrix.reshape(NH, fb, hu), up_matrix.reshape(NH, fb, hu), down_matrix[0],
        )
    ])
    ig, rg, gate_out, up_out, down_out = pl.pallas_call(
        copy_out,
        name="copy_out",
        out_shape=shapes,
        in_specs=[vm_spec] * 5,
        out_specs=(hbm_spec,) * 5,
        scratch_shapes=[dma((5,))],
        compiler_params=pltpu.CompilerParams(vmem_limit_bytes=1024 * 1024),
    )(*[pltpu.with_memory_space_constraint(a, pltpu.VMEM) for a in held])
    return (ig, rg.T, gate_out[None], up_out[None], down_out[None])


def solution(mesh):
    in_specs = (
        P("tok", "hid"),
        P("tok", "hid"),
        P("tok", None),
        P("tok", None),
        P("tok", None, "hid"),
        P("tok", None, "hid"),
        P("tok", "hid", None),
    )
    out_specs = (
        P("tok", "hid"),
        P("tok", None),
        P("tok", None, "hid"),
        P("tok", None, "hid"),
        P("tok", "hid", None),
    )
    return jax.shard_map(
        per_device, mesh=mesh, in_specs=in_specs, out_specs=out_specs, check_vma=False
    )
```

time: 90.7 us -> 86.4 us (0.953)
  Pallas kernels: 90 us -> 85.6 us
    pallas_call x1, Pallas kernels: 85.2 us -> 80.9 us  [per_device(): pl.pallas_call(exchange, name='exchange', out_shape=tuple((vmem(s.shape,...]
where the time goes in v3:
time: 86.4 us; the launch traced here: 86.3 us
  Pallas kernels  85.6 us (99%)
    pallas_call x1, Pallas kernels, per_device(): pl.pallas_call(exchange, name='exchange', out_shape=tuple((vmem(s.shape,...  80.9 us
    pallas_call x1, Pallas kernels, per_device(): pl.pallas_call(copy_out, name='copy_out', out_shape=shapes, in_specs=[vm_...  4.73 us

profile of v3, /device:TPU:1, one launch (start us, length us, event | category | flops | bytes accessed | tf_op | source)
XLA Modules:
  0.0 86.3 jit_solution(8416328000724743083)
XLA Ops:
  0.6 80.9 %exchange.1 = (bf16[128,256]{1,0:T(8,128)(2,1)S(1)}, bf16[2,128]{1,0:T(2,128)(2,1)S(1)}, bf16[4096,512]{1,0:T(8,128)(2,1)S(1)}, bf16[4096,512]{1,0:T(8,128)(2,1)S(1)}, bf16[512,4096]{1,0:T(8,128)(2,1)S(1)}) custom-call(s32[2,128]{1,0:T(2,128)} %bitcast.12, bf16[2,128]{1,0:T(2,128)(2,1)} %bitcast.13, bf16[128,256]{1,0:T(8,128)(2,1)} %tok_hbm.1, ...), custom_call_target="tpu_custom_call" | custom-call | tf_op jit(solution)/shard_map/exchange/pallas_call | solution.py:531
  81.5 4.7 %copy_out.1 = (bf16[128,256]{1,0:T(8,128)(2,1)}, bf16[2,128]{1,0:T(2,128)(2,1)}, bf16[4096,512]{1,0:T(8,128)(2,1)}, bf16[4096,512]{1,0:T(8,128)(2,1)}, bf16[512,4096]{1,0:T(8,128)(2,1)}) custom-call(bf16[128,256]{1,0:T(8,128)(2,1)S(1)} %get-tuple-element.15.refs_0_, bf16[2,128]{1,0:T(2,128)(2,1)S(1)} %get-tuple-element.16.refs_1_, ...), custom_call_target="tpu_custom_call" | custom-call | tf_op jit(solution)/shard_map/copy_out/pallas_call | solution.py:574

commit v4 on v3

--- a/solution.py
+++ b/solution.py
@@ -11,7 +11,11 @@
 NT = 8
 NH = 16
 SIGN = (1, -1)
-PARTNERS = ((0, 1), (2, 0), (2, 1), (1, 0), (1, 1), (3, 0), (3, 1))
+PARTNERS = ((0, 1), (1, 0), (1, 1), (3, 0), (3, 1), (2, 0), (2, 1))
+PLACE = (0, 1, 3, 2)
+RELAYS = (
+    ((0, 0, 0), (1, 0, 0)), ((0, 1, 0),), ((1, 1, 0),), ((0, 0, 1),), ((1, 0, 1),), ((0, 1, 1),), ((1, 1, 1),),
+)
 
 
 def dot(a, b):
@@ -47,8 +51,7 @@
     ids_ref, rw_ref, tok_ref, og_ref, wg, wu, wd, sel, selt, pack, psend, precv, xg, xt, acc_g, acc_u, acc_r,
     dd, hp, hpt, qs, q1, q2, qt, qb,
     e32, rl1s, rl1r, fn1s, fn1r, rl2s, rl2r, fn2s, fn2r, shr, rb,
-    w_sem, zs, zr, gs, gr, r1s, r1r, f1s, f1r, r2s, r2r, f2s, f2r,
-    qss, qsr, bs, br, cs, cr,
+    w_sem, zs, zr, gs, gr, gf, r1s, r1r, f1r, r2r, f2r, qss, qsr, bs, br,
 ):
     t = lax.axis_index("tok")
     hid = lax.axis_index("hid")
@@ -141,24 +144,26 @@
 
     def z_send(a, m):
         to = partner(m, False)
-        place = 2 * ((4 - PARTNERS[m][0]) % 4) + core
+        place = 2 * PLACE[-PARTNERS[m][0] % 4] + core
         if a == 2:
-            return to_tok(psend.at[to], precv.at[place], zs.at[2, m], zr.at[2, m], to)
-        return to_tok(pack.at[a, to], xg.at[a, hid, place], zs.at[a, m], zr.at[a, m], to)
-
-    def z_recv(a, m):
-        frm = partner(m, True)
-        place = 2 * ((4 - PARTNERS[m][0]) % 4) + lax.rem(core + PARTNERS[m][1], 2)
-        if a == 2:
-            return to_tok(psend.at[frm], precv.at[place], zs.at[2, m], zr.at[2, m], frm)
-        return to_tok(pack.at[a, frm], xg.at[a, hid, place], zs.at[a, m], zr.at[a, m], frm)
-
-    z_send(0, 0).start()
-    z_send(1, 0).start()
-    for a in range(3):
-        for m in range(7):
-            if a == 2 or m > 0:
+            return to_tok(psend.at[to], precv.at[place], zs.at[1], zr.at[2, 0], to)
+        return to_tok(pack.at[a, to], xg.at[a, hid, place], zs.at[0], zr.at[a, (m + 3) // 4], to)
+
+    def z_recv(a, group):
+        first, count = ((0, 1), (2, 4), (6, 2))[group]
+        ref = xg.at[a, hid, pl.ds(1 - core if group == 0 else first, count)]
+        return to_tok(ref, ref, zs.at[0], zr.at[a, group], partner(0, True))
+
+    def p_recv():
+        ref = precv.at[pl.ds(0, 7)]
+        return to_tok(ref, ref, zs.at[1], zr.at[2, 0], partner(0, True))
+
+    for group in ((0,), (1, 2, 3, 4), (5, 6)):
+        for a in range(2):
+            for m in group:
                 z_send(a, m).start()
+    for m in range(7):
+        z_send(2, m).start()
 
     prim = (cx, cy)
     seco = (cy, cx)
@@ -167,13 +172,17 @@
         return 4 * p + s if a == 0 else 4 * s + p
 
     half = NT // 2
-    span = {(0, None): (0, 2), (0, 0): (0, 1), (0, 1): (1, 1),
-            (1, None): (2, 6), (1, 0): (2, 3), (1, 1): (5, 3)}
+    span = {}
+    for w, (first, count) in enumerate(((0, 2), (2, 4), (6, 2))):
+        span[w, None] = (first, count)
+        span[w, 0] = (first, count // 2)
+        span[w, 1] = (first + count // 2, count // 2)
 
     def gather_copy(a, w, block, h, sem, target):
         first, count = span[w, h]
         ref = xg.at[a, block, pl.ds(first, count)]
-        return to_hid(ref, ref, gs.at[w, a, sem], gr.at[w, a, sem], target)
+        rsem = gr.at[w, a, sem] if sem < 11 else gf.at[a, sem - 11]
+        return to_hid(ref, ref, gs.at[0], rsem, target)
 
     def p_own(a, w, d, recv=False):
         p, s = prim[a], seco[a]
@@ -183,17 +192,17 @@
     def p_fwd(a, w, d, recv=False):
         p, s = prim[a], seco[a]
         b = blk(a, m4(p - 2 * SIGN[d]) if recv else m4(p - SIGN[d]), s)
-        return gather_copy(a, w, b, d, 2 + d, blk(a, m4(p + SIGN[d]), s))
+        return gather_copy(a, w, b, d, 2, blk(a, m4(p + SIGN[d]), s))
 
     def s_own(a, w, o, d, recv=False):
         p, s = prim[a], seco[a]
         b = blk(a, m4(p + o), m4(s - SIGN[d]) if recv else s)
-        return gather_copy(a, w, b, None, 4 + 2 * o + d, blk(a, p, m4(s + SIGN[d])))
+        return gather_copy(a, w, b, None, 3 + 2 * o + d, blk(a, p, m4(s + SIGN[d])))
 
     def s_fwd(a, w, o, d, recv=False):
         p, s = prim[a], seco[a]
         b = blk(a, m4(p + o), m4(s - 2 * SIGN[d]) if recv else m4(s - SIGN[d]))
-        return gather_copy(a, w, b, d, 12 + 2 * o + d, blk(a, p, m4(s + SIGN[d])))
+        return gather_copy(a, w, b, d, 11 + o, blk(a, p, m4(s + SIGN[d])))
 
     def gather_begin(w, a):
         for d in range(2):
@@ -211,10 +220,15 @@
             s_fwd(a, w, 0, d).start()
 
     def gather_5(w, a):
-        for d in range(2):
-            p_fwd(a, w, d, True).wait_recv()
+        p, s = prim[a], seco[a]
+        gather_copy(a, w, blk(a, m4(p + 2), s), None, 2, blk(a, m4(p + 1), s)).wait_recv()
         for d in range(2):
             s_own(a, w, 2, d).start()
+
+    def gather_end(a, o):
+        p, s = prim[a], seco[a]
+        ref = xg.at[a, blk(a, m4(p + o), m4(s + 2))]
+        to_hid(ref, ref, gs.at[0], gf.at[a, o], blk(a, p, m4(s + 1))).wait_recv()
 
     def gather_pass(w, a, o):
         for d in range(2):
@@ -231,18 +245,19 @@
     for a in range(2):
         gather_1(0, a)
     for a in range(2):
+        z_recv(a, 1).wait_recv()
+        gather_begin(1, a)
+    for a in range(2):
         gather_5(0, a)
-    for a in range(2):
-        for m in range(1, 7):
-            z_recv(a, m).wait_recv()
-        gather_begin(1, a)
     for a in range(2):
         for o in (3, 1):
             gather_pass(0, a, o)
     for a in range(2):
+        z_recv(a, 2).wait_recv()
+        gather_begin(2, a)
+    for a in range(2):
         gather_pass(0, a, 2)
-    for m in range(7):
-        z_recv(2, m).wait_recv()
+    p_recv().wait_recv()
     for c in w_copies:
         c.wait()
 
@@ -252,32 +267,34 @@
     def gather_step(j):
         @pl.when(j == 1)
         def _():
-            for a in range(2):
-                gather_1(1, a)
+            for w in (1, 2):
+                for a in range(2):
+                    gather_1(w, a)
 
         @pl.when(j == 5)
         def _():
-            for a in range(2):
-                gather_5(1, a)
+            for w in (1, 2):
+                for a in range(2):
+                    gather_5(w, a)
 
         @pl.when(j == 6)
         def _():
-            for a in range(2):
-                for o in (3, 1):
-                    gather_pass(1, a, o)
+            for w in (1, 2):
+                for a in range(2):
+                    for o in (3, 1):
+                        gather_pass(w, a, o)
 
         @pl.when(j == 10)
         def _():
-            for a in range(2):
-                gather_pass(1, a, 2)
+            for w in (1, 2):
+                for a in range(2):
+                    gather_pass(w, a, 2)
 
         for n, o in ((12, 0), (13, 3), (14, 1), (15, 2)):
             @pl.when(j == n)
             def _():
                 for a in range(2):
-                    for w in range(2):
-                        for d in range(2):
-                            s_fwd(a, w, o, d, True).wait_recv()
+                    gather_end(a, o)
 
         o = pick(j, o_of)
         q = pick(j, q_of)
@@ -288,6 +305,9 @@
         acc_u[...] += dot(x, wu[bx])
         acc_r[...] += dot_nt(xg[1, bg].reshape(rows, fb), wd[:, pl.ds(pl.multiple_of(bg * fb, fb), fb)])
         xt[bx] = x.T
+        for w in (wg, wu):
+            for k in range(hu // fb):
+                w[bx, :, k * fb : (k + 1) * fb] = w[bx, :, k * fb : (k + 1) * fb].T
 
     loop(0, NH, gather_step)
 
@@ -320,44 +340,45 @@
         return blk(a, p, m4(s + SIGN[d]))
 
     def rl1(a, d, i):
-        return to_hid(rl1s.at[a, d, i], rl1r.at[a, d, i], r1s.at[a, d, i], r1r.at[a, d, i], along(a, d))
+        return to_hid(rl1s.at[a, d, i], rl1r.at[a, d, i], r1s.at[0], r1r.at[a, d, i], along(a, d))
 
     def fn1(a, d, q):
-        return to_hid(fn1s.at[a, d, q], fn1r.at[a, d, q], f1s.at[a, d, q], f1r.at[a, d, q], along(a, d))
+        return to_hid(fn1s.at[a, d, q], fn1r.at[a, q, d], r1s.at[1], f1r.at[a, q], along(a, d))
 
     def rl2(a, d):
-        return to_hid(rl2s.at[a, d], rl2r.at[a, d], r2s.at[a, d], r2r.at[a, d], across(a, d))
+        return to_hid(rl2s.at[a, d], rl2r.at[a, d], r1s.at[2], r2r.at[a, d], across(a, d))
 
     def fn2(a, d):
-        return to_hid(fn2s.at[a, d], fn2r.at[a, d], f2s.at[a, d], f2r.at[a, d], across(a, d))
-
-    def q_x(k, recv=False):
-        frm = m4(cx - k) if recv else cx
-        return to_hid(qs, q1.at[frm], qss.at[0, k], qsr.at[0, k], 4 * m4(cx + k) + cy)
-
-    def q_y(k, recv=False):
-        frm = m4(cy - k) if recv else cy
-        return to_hid(qt, q2.at[frm], qss.at[1, k], qsr.at[1, k], 4 * cx + m4(cy + k))
+        return to_hid(fn2s.at[a, d], fn2r.at[a, d], r1s.at[3], f2r.at[a], across(a, d))
+
+    def q_x(k):
+        return to_hid(qs, q1.at[cx], qss.at[0], qsr.at[0], 4 * m4(cx + k) + cy)
+
+    def q_y(k):
+        return to_hid(qt, q2.at[cy], qss.at[1], qsr.at[1], 4 * cx + m4(cy + k))
 
     x_of = (2, 2, 3, 2, 1, 2, 0, 1, 3, 3, 1, 1, 3, 0, 0, 0)
     y_of = (2, 3, 2, 1, 2, 0, 2, 3, 3, 1, 1, 0, 0, 1, 3, 0)
 
     def e_step(n):
-        h = 4 * m4(cx + pick(n, x_of)) + m4(cy + pick(n, y_of))
-        e = dot_nt(dd[:, 0:hu], wg[h]) + dot_nt(dd[:, hu : 2 * hu], wu[h])
-        e32[h] = e.reshape(2, hrows, fb)
-        for k, (d, i) in ((0, (0, 0)), (1, (1, 0)), (3, (0, 1)), (5, (1, 1))):
-            for a in range(2):
-                @pl.when(n == (k + a if k else 0))
-                def _():
-                    rl1s[a, d, i] = e32[h, a].astype(BF)
+        where = []
+        for k in range(2):
+            h = 4 * m4(cx + pick(2 * n + k, x_of)) + m4(cy + pick(2 * n + k, y_of))
+            turned = jnp.concatenate(
+                [w[h, :, i * fb : (i + 1) * fb] for w in (wg, wu) for i in range(hu // fb)], axis=0)
+            where.append(h)
+            e32[h] = dot(dd[...], turned).reshape(2, hrows, fb)
+        for k, todo in enumerate(RELAYS):
+            @pl.when(n == k // 2)
+            def _():
+                for a, d, i in todo:
+                    rl1s[a, d, i] = e32[where[k % 2], a].astype(BF)
                     rl1(a, d, i).start()
-
-    loop(0, NH, e_step)
 
     q1[cx] = qs[...]
     for k in range(1, 4):
         q_x(k).start()
+    loop(0, NH // 2, e_step)
 
     relayed = {2: (0, 0), 1: (0, 1), 3: (1, 0), 0: (1, 1)}
 
@@ -373,10 +394,9 @@
                 fn1(a, d, q).start()
 
     def total_of(a, q):
-        for d in range(2):
-            fn1(a, d, q).wait_recv()
+        to_hid(fn1r.at[a, q], fn1r.at[a, q], r1s.at[1], f1r.at[a, q], along(a, 0)).wait_recv()
         return (e32[blk(a, prim[a], m4(seco[a] + q)), a]
-                + fn1r[a, 0, q].astype(F32) + fn1r[a, 1, q].astype(F32))
+                + fn1r[a, q, 0].astype(F32) + fn1r[a, q, 1].astype(F32))
 
     hpt[...] = hp[...].T
 
@@ -392,8 +412,7 @@
 
     first_step(2)
     first_step(3)
-    for k in range(1, 4):
-        q_x(k, True).wait_recv()
+    to_hid(q1.at[pl.ds(0, 3)], q1.at[pl.ds(0, 3)], qss.at[0], qsr.at[0], along(0, 0)).wait_recv()
     qt[...] = q1[0] + q1[1] + q1[2] + q1[3]
     q2[cy] = qt[...]
     for k in range(1, 4):
@@ -409,8 +428,7 @@
             rl2(a, d).start()
     first_step(0)
     loop(3, 6, weight_step)
-    for k in range(1, 4):
-        q_y(k, True).wait_recv()
+    to_hid(q2.at[pl.ds(0, 3)], q2.at[pl.ds(0, 3)], qss.at[1], qsr.at[1], across(0, 0)).wait_recv()
     qw = q2[0] + q2[1] + q2[2] + q2[3]
     qsum = qb.at[NT]
     qsum[...] = qw
@@ -418,11 +436,7 @@
 
     def c_send(m):
         to = partner(m, False)
-        return to_tok(qb.at[NT], qb.at[t], cs.at[m], cr.at[m], to)
-
-    def c_recv(m):
-        frm = partner(m, True)
-        return to_tok(qb.at[NT], qb.at[frm], cs.at[m], cr.at[m], frm)
+        return to_tok(qb.at[NT], qb.at[t], bs.at[1], br.at[1], to)
 
     for m in range(7):
         c_send(m).start()
@@ -442,62 +456,56 @@
     def b_send(m):
         to = partner(m, False)
         dz, dc = PARTNERS[m]
-        return to_tok(shr.at[2 * dz + lax.rem(core + dc, 2)], rb.at[t], bs.at[m], br.at[m], to)
-
-    def b_recv(m):
-        frm = partner(m, True)
-        return to_tok(shr.at[0], rb.at[frm], bs.at[m], br.at[m], frm)
+        return to_tok(shr.at[2 * PLACE[dz] + lax.rem(core + dc, 2)], rb.at[t], bs.at[0], br.at[0], to)
 
     for a in (1, 0):
         s = total_of(a, 0)
+        to_hid(fn2r.at[a], fn2r.at[a], r1s.at[3], f2r.at[a], across(a, 0)).wait_recv()
         for d in range(2):
-            fn2(a, d).wait_recv()
             s = s + fn2r[a, d].astype(F32).reshape(hrows, fb)
         shr[a * half : (a + 1) * half] = s.astype(BF).reshape(half, cap, fb)
         for m, (dz, dc) in enumerate(PARTNERS):
-            if dz // 2 == a:
+            if PLACE[dz] // 2 == a:
                 b_send(m).start()
     rb[t] = shr[core]
 
-    for m in range(7):
-        c_recv(m).wait_recv()
+    def back_wait(ref, k):
+        ref = ref.at[pl.ds(0, len(PARTNERS))]
+        return to_tok(ref, ref, bs.at[k], br.at[k], partner(0, True))
+
+    back_wait(qb, 1).wait_recv()
     block = lax.broadcasted_iota(I32, (8, n_tok), 0)
     zero = jnp.zeros((1, n_tok), F32)
     route = [zero, zero]
     for e in range(NT):
-        row = jnp.sum(jnp.where(block == 2 * m4(z - e // 2) + core, qb[e], 0.0), axis=0, keepdims=True)
+        row = jnp.sum(jnp.where(block == 2 * pick(m4(z - e // 2), PLACE) + core, qb[e], 0.0), axis=0, keepdims=True)
         col = jnp.sum(jnp.where(diag, row, 0.0), axis=1, keepdims=True)
         val = jnp.sum(sel[e] * col, axis=0, keepdims=True)
         for k in range(2):
             route[k] = route[k] + jnp.where(ids[k : k + 1, :] == e, val, 0.0)
     rg_ref[...] = jnp.concatenate(route, axis=0).astype(BF)
 
-    for m in range(7):
-        b_recv(m).wait_recv()
+    back_wait(rb, 0).wait_recv()
     ig_ref[...] = dot(selt[...].astype(BF), rb[...].reshape(rows, fb)).astype(BF)
 
-    for m in range(7):
-        for a in range(3):
-            z_send(a, m).wait_send()
-        c_send(m).wait_send()
-        b_send(m).wait_send()
-    for k in range(1, 4):
-        q_x(k).wait_send()
-        q_y(k).wait_send()
-    for a in range(2):
-        for d in range(2):
-            for w in range(2):
-                p_own(a, w, d).wait_send()
-                p_fwd(a, w, d).wait_send()
-                for o in range(4):
-                    s_own(a, w, o, d).wait_send()
-                    s_fwd(a, w, o, d).wait_send()
-            for i in range(2):
-                rl1(a, d, i).wait_send()
-            for q in range(4):
-                fn1(a, d, q).wait_send()
-            rl2(a, d).wait_send()
-            fn2(a, d).wait_send()
+    n_z = len(PARTNERS)
+    near = partner(0, False)
+    beside = along(0, 0)
+    ends = [
+        to_tok(pack.at[:, pl.ds(0, n_z)], pack.at[:, pl.ds(0, n_z)], zs.at[0], zr.at[0, 0], near),
+        to_tok(psend.at[pl.ds(0, n_z)], psend.at[pl.ds(0, n_z)], zs.at[1], zr.at[0, 0], near),
+        to_hid(xg.at[:, pl.ds(0, NH - 1)], xg.at[:, pl.ds(0, NH - 1)], gs.at[0], gf.at[0, 0], beside),
+        to_hid(rl1s, rl1r, r1s.at[0], gf.at[0, 0], beside),
+        to_hid(fn1s, fn1s, r1s.at[1], gf.at[0, 0], beside),
+        to_hid(rl2s, rl2r, r1s.at[2], gf.at[0, 0], beside),
+        to_hid(fn2s, fn2r, r1s.at[3], gf.at[0, 0], beside),
+        to_hid(q1.at[pl.ds(0, 3)], q1.at[pl.ds(0, 3)], qss.at[0], gf.at[0, 0], beside),
+        to_hid(q2.at[pl.ds(0, 3)], q2.at[pl.ds(0, 3)], qss.at[1], gf.at[0, 0], beside),
+        back_wait(shr, 0),
+        back_wait(qb, 1),
+    ]
+    for c in ends:
+        c.wait_send()
 
 
 def copy_out(*refs):
@@ -546,20 +554,15 @@
             vmem((8, n_tok), F32), vmem((NT + 1, 8, n_tok), F32),
             vmem((NH, 2, hr, fb), F32),
             vmem((2, 2, 2, hr, fb), BF), vmem((2, 2, 2, hr, fb), BF),
-            vmem((2, 2, 4, hr, fb), BF), vmem((2, 2, 4, hr, fb), BF),
+            vmem((2, 2, 4, hr, fb), BF), vmem((2, 4, 2, hr, fb), BF),
             vmem((2, 2, hr // 2, fb), BF), vmem((2, 2, hr // 2, fb), BF),
             vmem((2, 2, 2, hr // 2, fb), BF), vmem((2, 2, 2, hr // 2, fb), BF),
             vmem((NT, cap, fb), BF), vmem((NT, cap, fb), BF),
             dma((7,)),
-            dma((3, NT)), dma((3, NT)),
-            dma((2, 2, 20)), dma((2, 2, 20)),
-            dma((2, 2, 2)), dma((2, 2, 2)),
-            dma((2, 2, 4)), dma((2, 2, 4)),
-            dma((2, 2)), dma((2, 2)),
-            dma((2, 2)), dma((2, 2)),
-            dma((2, 4)), dma((2, 4)),
-            dma((NT,)), dma((NT,)),
-            dma((NT,)), dma((NT,)),
+            dma((2,)), dma((3, 3)),
+            dma((1,)), dma((3, 2, 11)), dma((2, 4)),
+            dma((4,)), dma((2, 2, 2)), dma((2, 4)), dma((2, 2)), dma((2,)),
+            dma((2,)), dma((2,)), dma((2,)), dma((2,)),
         ],
         compiler_params=pltpu.CompilerParams(
             collective_id=0, has_side_effects=True, vmem_limit_bytes=46 * 1024 * 1024

time: 86.4 us -> 77.1 us (0.89)
  Pallas kernels: 85.6 us -> 76.3 us
    pallas_call x1, Pallas kernels: 80.9 us -> 71.6 us  [per_device(): pl.pallas_call(exchange, name='exchange', out_shape=tuple((vmem(s.shape,...]
where the time goes in v4:
time: 77.1 us; the launch traced here: 76.9 us
  Pallas kernels  76.3 us (99%)
    pallas_call x1, Pallas kernels, per_device(): pl.pallas_call(exchange, name='exchange', out_shape=tuple((vmem(s.shape,...  71.6 us
    pallas_call x1, Pallas kernels, per_device(): pl.pallas_call(copy_out, name='copy_out', out_shape=shapes, in_specs=[vm_...  4.73 us

profile of v4, /device:TPU:1, one launch (start us, length us, event | category | flops | bytes accessed | tf_op | source)
XLA Modules:
  0.0 76.9 jit_solution(17230538040030596148)
XLA Ops:
  0.6 71.6 %exchange.1 = (bf16[128,256]{1,0:T(8,128)(2,1)S(1)}, bf16[2,128]{1,0:T(2,128)(2,1)S(1)}, bf16[4096,512]{1,0:T(8,128)(2,1)S(1)}, bf16[4096,512]{1,0:T(8,128)(2,1)S(1)}, bf16[512,4096]{1,0:T(8,128)(2,1)S(1)}) custom-call(s32[2,128]{1,0:T(2,128)} %bitcast.12, bf16[2,128]{1,0:T(2,128)(2,1)} %bitcast.13, bf16[128,256]{1,0:T(8,128)(2,1)} %tok_hbm.1, ...), custom_call_target="tpu_custom_call" | custom-call | tf_op jit(solution)/shard_map/exchange/pallas_call | solution.py:539
  72.2 4.7 %copy_out.1 = (bf16[128,256]{1,0:T(8,128)(2,1)}, bf16[2,128]{1,0:T(2,128)(2,1)}, bf16[4096,512]{1,0:T(8,128)(2,1)}, bf16[4096,512]{1,0:T(8,128)(2,1)}, bf16[512,4096]{1,0:T(8,128)(2,1)}) custom-call(bf16[128,256]{1,0:T(8,128)(2,1)S(1)} %get-tuple-element.15.refs_0_, bf16[2,128]{1,0:T(2,128)(2,1)S(1)} %get-tuple-element.16.refs_1_, ...), custom_call_target="tpu_custom_call" | custom-call | tf_op jit(solution)/shard_map/copy_out/pallas_call | solution.py:577

commit v5 on v4

--- a/solution.py
+++ b/solution.py
@@ -13,6 +13,8 @@
 SIGN = (1, -1)
 PARTNERS = ((0, 1), (1, 0), (1, 1), (3, 0), (3, 1), (2, 0), (2, 1))
 PLACE = (0, 1, 3, 2)
+STREAMS = ((0, 0, 2, 0), (0, 2, 4, 0), (0, 6, 2, 1), (1, 6, 2, 1), (2, 0, 128, 1))
+X_OWN, X_NEXT, X_FAR, G_FAR, RAW = range(5)
 RELAYS = (
     ((0, 0, 0), (1, 0, 0)), ((0, 1, 0),), ((1, 1, 0),), ((0, 0, 1),), ((1, 0, 1),), ((0, 1, 1),), ((1, 1, 1),),
 )
@@ -48,10 +50,10 @@
 def exchange(
     ids_hbm, rw_hbm, tok_hbm, og_hbm, wg_hbm, wu_hbm, wd_hbm,
     ig_ref, rg_ref, gate_ref, up_ref, down_ref,
-    ids_ref, rw_ref, tok_ref, og_ref, wg, wu, wd, sel, selt, pack, psend, precv, xg, xt, acc_g, acc_u, acc_r,
+    ids_ref, rw_ref, tok_ref, raw, wg, wu, wd, sel, picks, selt, pack, pk, psend, precv, xg, xt, acc_g, acc_u, acc_r,
     dd, hp, hpt, qs, q1, q2, qt, qb,
     e32, rl1s, rl1r, fn1s, fn1r, rl2s, rl2r, fn2s, fn2r, shr, rb,
-    w_sem, zs, zr, gs, gr, gf, r1s, r1r, f1r, r2r, f2r, qss, qsr, bs, br,
+    w_sem, zs, zr, zg, gs, gr, gf, r1s, r1r, f1r, r2r, f2r, qss, qsr, bs, br,
 ):
     t = lax.axis_index("tok")
     hid = lax.axis_index("hid")
@@ -79,7 +81,7 @@
     small = [
         pltpu.make_async_copy(src, dst, w_sem.at[3 + k])
         for k, (src, dst) in enumerate(
-            ((ids_hbm, ids_ref), (rw_hbm, rw_ref), (tok_hbm, tok_ref), (og_hbm, og_ref))
+            ((ids_hbm, ids_ref), (rw_hbm, rw_ref), (tok_hbm, tok_ref), (og_hbm, raw.at[hid]))
         )
     ]
     for c in small:
@@ -128,12 +130,9 @@
         col = jnp.sum(one * weight[e : e + 1, :], axis=1, keepdims=True)
         row = jnp.sum(jnp.where(diag, col, 0.0), axis=0, keepdims=True)
         psend[e] = jnp.broadcast_to(row, (8, n_tok))
-    picks = sel[...].reshape(rows, n_tok)
-    picks_bf = picks.astype(BF)
-    pack[0] = dot(picks_bf, tok_ref[...]).astype(BF).reshape(NT, cap, fb)
-    pack[1] = dot(picks_bf, og_ref[...]).astype(BF).reshape(NT, cap, fb)
-    xg[0, hid, core] = pack[0, t]
-    xg[1, hid, core] = pack[1, t]
+    picks[...] = sel[...].reshape(rows, n_tok).astype(BF)
+    pack[...] = dot(picks[...], tok_ref[...]).astype(BF).reshape(NT, cap, fb)
+    xg[0, hid, core] = pack[t]
     precv[core] = psend[t]
 
     pl.semaphore_wait(bar, len(PARTNERS) + 6)
@@ -145,9 +144,11 @@
     def z_send(a, m):
         to = partner(m, False)
         place = 2 * PLACE[-PARTNERS[m][0] % 4] + core
+        group = (m + 3) // 4
         if a == 2:
             return to_tok(psend.at[to], precv.at[place], zs.at[1], zr.at[2, 0], to)
-        return to_tok(pack.at[a, to], xg.at[a, hid, place], zs.at[0], zr.at[a, (m + 3) // 4], to)
+        src = pack.at[to] if a == 0 else pk.at[hid, to]
+        return to_tok(src, xg.at[a, hid, place], zs.at[3 * a], zr.at[a, group], to)
 
     def z_recv(a, group):
         first, count = ((0, 1), (2, 4), (6, 2))[group]
@@ -158,158 +159,185 @@
         ref = precv.at[pl.ds(0, 7)]
         return to_tok(ref, ref, zs.at[1], zr.at[2, 0], partner(0, True))
 
-    for group in ((0,), (1, 2, 3, 4), (5, 6)):
-        for a in range(2):
-            for m in group:
-                z_send(a, m).start()
+    prim = (cx, cy)
+    seco = (cy, cx)
+
+    def blk(a, p, s):
+        return 4 * p + s if a == 0 else 4 * s + p
+
+    half = NT // 2
+
+    def part(st, block, h=None):
+        array, first, count = STREAMS[st][:3]
+        if h is not None:
+            count //= 2
+            first += h * count
+        base = raw.at[block] if array == 2 else xg.at[array, block]
+        return base.at[pl.ds(first, count)]
+
+    def gather_copy(st, block, h, sem, target):
+        ref = part(st, block, h)
+        rsem = gr.at[st, sem] if sem < 11 else gf.at[st, sem - 11]
+        return to_hid(ref, ref, gs.at[STREAMS[st][0]], rsem, target)
+
+    def frame(st):
+        g = STREAMS[st][3]
+        return g, prim[g], seco[g]
+
+    def p_own(st, d, recv=False):
+        g, p, s = frame(st)
+        b = blk(g, m4(p - SIGN[d]) if recv else p, s)
+        return gather_copy(st, b, None, d, blk(g, m4(p + SIGN[d]), s))
+
+    def p_fwd(st, d):
+        g, p, s = frame(st)
+        return gather_copy(st, blk(g, m4(p - SIGN[d]), s), d, 2, blk(g, m4(p + SIGN[d]), s))
+
+    def s_own(st, o, d, recv=False):
+        g, p, s = frame(st)
+        b = blk(g, m4(p + o), m4(s - SIGN[d]) if recv else s)
+        return gather_copy(st, b, None, 3 + 2 * o + d, blk(g, p, m4(s + SIGN[d])))
+
+    def s_fwd(st, o, d):
+        g, p, s = frame(st)
+        return gather_copy(st, blk(g, m4(p + o), m4(s - SIGN[d])), d, 11 + o, blk(g, p, m4(s + SIGN[d])))
+
+    def gather_begin(st):
+        for d in range(2):
+            p_own(st, d).start()
+            s_own(st, 0, d).start()
+
+    def gather_1(st):
+        for d in range(2):
+            p_own(st, d, True).wait_recv()
+            p_fwd(st, d).start()
+            for d2 in range(2):
+                s_own(st, (4 - SIGN[d]) % 4, d2).start()
+        for d in range(2):
+            s_own(st, 0, d, True).wait_recv()
+            s_fwd(st, 0, d).start()
+
+    def gather_5(st):
+        g, p, s = frame(st)
+        gather_copy(st, blk(g, m4(p + 2), s), None, 2, blk(g, m4(p + 1), s)).wait_recv()
+        for d in range(2):
+            s_own(st, 2, d).start()
+
+    def gather_pass(st, *offsets):
+        for o in offsets:
+            for d in range(2):
+                s_own(st, o, d, True).wait_recv()
+                s_fwd(st, o, d).start()
+
+    def gather_end(st, *offsets):
+        g, p, s = frame(st)
+        for o in offsets:
+            gather_copy(st, blk(g, m4(p + o), m4(s + 2)), None, 11 + o, blk(g, p, m4(s + 1))).wait_recv()
+
+    o_of = (0, 3, 1, 0, 0, 3, 3, 1, 1, 2, 0, 2, 3, 2, 1, 2)
+    q_of = (0, 0, 0, 3, 1, 3, 1, 3, 1, 0, 2, 3, 2, 1, 2, 2)
+
+    def raw_block(n):
+        return blk(1, m4(cy + pick(n, o_of)), m4(cx + pick(n, q_of)))
+
+    def raw_pack(n):
+        h = raw_block(n)
+        pk[h] = dot(picks[...], raw[h]).astype(BF).reshape(NT, cap, fb)
+        xg[1, h, core] = pk[h, t]
+        for m in range(5):
+            to = partner(m, False)
+            place = 2 * PLACE[-PARTNERS[m][0] % 4] + core
+            to_tok(pk.at[h, to], xg.at[1, h, place], zs.at[2], zg.at[n], to).start()
+
+    def raw_packs(*places):
+        loop(0, len(places), lambda i: raw_pack(pick(i, places)))
+
+    gather_begin(RAW)
+    for m in range(5):
+        z_send(0, m).start()
+    raw_pack(0)
+    for a in range(2):
+        for m in (5, 6):
+            z_send(a, m).start()
     for m in range(7):
         z_send(2, m).start()
-
-    prim = (cx, cy)
-    seco = (cy, cx)
-
-    def blk(a, p, s):
-        return 4 * p + s if a == 0 else 4 * s + p
-
-    half = NT // 2
-    span = {}
-    for w, (first, count) in enumerate(((0, 2), (2, 4), (6, 2))):
-        span[w, None] = (first, count)
-        span[w, 0] = (first, count // 2)
-        span[w, 1] = (first + count // 2, count // 2)
-
-    def gather_copy(a, w, block, h, sem, target):
-        first, count = span[w, h]
-        ref = xg.at[a, block, pl.ds(first, count)]
-        rsem = gr.at[w, a, sem] if sem < 11 else gf.at[a, sem - 11]
-        return to_hid(ref, ref, gs.at[0], rsem, target)
-
-    def p_own(a, w, d, recv=False):
-        p, s = prim[a], seco[a]
-        b = blk(a, m4(p - SIGN[d]) if recv else p, s)
-        return gather_copy(a, w, b, None, d, blk(a, m4(p + SIGN[d]), s))
-
-    def p_fwd(a, w, d, recv=False):
-        p, s = prim[a], seco[a]
-        b = blk(a, m4(p - 2 * SIGN[d]) if recv else m4(p - SIGN[d]), s)
-        return gather_copy(a, w, b, d, 2, blk(a, m4(p + SIGN[d]), s))
-
-    def s_own(a, w, o, d, recv=False):
-        p, s = prim[a], seco[a]
-        b = blk(a, m4(p + o), m4(s - SIGN[d]) if recv else s)
-        return gather_copy(a, w, b, None, 3 + 2 * o + d, blk(a, p, m4(s + SIGN[d])))
-
-    def s_fwd(a, w, o, d, recv=False):
-        p, s = prim[a], seco[a]
-        b = blk(a, m4(p + o), m4(s - 2 * SIGN[d]) if recv else m4(s - SIGN[d]))
-        return gather_copy(a, w, b, d, 11 + o, blk(a, p, m4(s + SIGN[d])))
-
-    def gather_begin(w, a):
-        for d in range(2):
-            p_own(a, w, d).start()
-            s_own(a, w, 0, d).start()
-
-    def gather_1(w, a):
-        for d in range(2):
-            p_own(a, w, d, True).wait_recv()
-            p_fwd(a, w, d).start()
-            for d2 in range(2):
-                s_own(a, w, (4 - SIGN[d]) % 4, d2).start()
-        for d in range(2):
-            s_own(a, w, 0, d, True).wait_recv()
-            s_fwd(a, w, 0, d).start()
-
-    def gather_5(w, a):
-        p, s = prim[a], seco[a]
-        gather_copy(a, w, blk(a, m4(p + 2), s), None, 2, blk(a, m4(p + 1), s)).wait_recv()
-        for d in range(2):
-            s_own(a, w, 2, d).start()
-
-    def gather_end(a, o):
-        p, s = prim[a], seco[a]
-        ref = xg.at[a, blk(a, m4(p + o), m4(s + 2))]
-        to_hid(ref, ref, gs.at[0], gf.at[a, o], blk(a, p, m4(s + 1))).wait_recv()
-
-    def gather_pass(w, a, o):
-        for d in range(2):
-            s_own(a, w, o, d, True).wait_recv()
-            s_fwd(a, w, o, d).start()
-
-    for a in range(2):
-        z_recv(a, 0).wait_recv()
-        gather_begin(0, a)
+    z_recv(0, 0).wait_recv()
+    gather_begin(X_OWN)
     acc_g[...] = jnp.zeros_like(acc_g)
     acc_u[...] = jnp.zeros_like(acc_u)
     acc_r[...] = jnp.zeros_like(acc_r)
-    selt[...] = picks.T
-    for a in range(2):
-        gather_1(0, a)
-    for a in range(2):
-        z_recv(a, 1).wait_recv()
-        gather_begin(1, a)
-    for a in range(2):
-        gather_5(0, a)
-    for a in range(2):
-        for o in (3, 1):
-            gather_pass(0, a, o)
-    for a in range(2):
-        z_recv(a, 2).wait_recv()
-        gather_begin(2, a)
-    for a in range(2):
-        gather_pass(0, a, 2)
-    p_recv().wait_recv()
+    selt[...] = sel[...].reshape(rows, n_tok).T
+    gather_1(RAW)
+    raw_packs(1, 2, 3, 4)
+    gather_1(X_OWN)
+    gather_5(RAW)
+    raw_packs(9)
+    gather_5(X_OWN)
+    gather_pass(RAW, 3, 1)
+    raw_packs(5, 6, 7, 8)
+    gather_pass(X_OWN, 3, 1)
+    gather_pass(RAW, 2)
+    z_recv(0, 1).wait_recv()
+    gather_begin(X_NEXT)
+    z_recv(0, 2).wait_recv()
+    gather_begin(X_FAR)
+    z_recv(1, 2).wait_recv()
+    gather_begin(G_FAR)
+    raw_packs(11, 13)
+    gather_pass(X_OWN, 2)
+    gather_end(RAW, 0, 3, 1, 2)
+    raw_packs(10, 12, 14, 15)
+    for st in (X_NEXT, X_FAR, G_FAR):
+        gather_1(st)
     for c in w_copies:
         c.wait()
-
-    o_of = (0, 3, 1, 0, 0, 2, 3, 3, 1, 1, 2, 2, 0, 3, 1, 2)
-    q_of = (0, 0, 0, 3, 1, 0, 3, 1, 3, 1, 3, 1, 2, 2, 2, 2)
+    gather_end(X_OWN, 0, 3, 1, 2)
 
     def gather_step(j):
-        @pl.when(j == 1)
+        @pl.when(j == 2)
         def _():
-            for w in (1, 2):
-                for a in range(2):
-                    gather_1(w, a)
-
-        @pl.when(j == 5)
+            for st in (X_NEXT, X_FAR, G_FAR):
+                gather_5(st)
+            for st in (X_NEXT, X_FAR, G_FAR):
+                gather_pass(st, 3, 1)
+
+        @pl.when(j == 4)
         def _():
-            for w in (1, 2):
-                for a in range(2):
-                    gather_5(w, a)
-
-        @pl.when(j == 6)
-        def _():
-            for w in (1, 2):
-                for a in range(2):
-                    for o in (3, 1):
-                        gather_pass(w, a, o)
-
-        @pl.when(j == 10)
-        def _():
-            for w in (1, 2):
-                for a in range(2):
-                    gather_pass(w, a, 2)
-
-        for n, o in ((12, 0), (13, 3), (14, 1), (15, 2)):
+            for st in (X_NEXT, X_FAR, G_FAR):
+                gather_pass(st, 2)
+
+        for n, near, far in ((4, (), (0,)), (5, (0,), (3,)), (6, (3,), (1,)), (7, (1, 2), (2,))):
             @pl.when(j == n)
             def _():
-                for a in range(2):
-                    gather_end(a, o)
-
-        o = pick(j, o_of)
-        q = pick(j, q_of)
-        bx = blk(0, m4(cx + o), m4(cy + q))
-        bg = blk(1, m4(cy + o), m4(cx + q))
-        x = xg[0, bx].reshape(rows, fb)
-        acc_g[...] += dot(x, wg[bx])
-        acc_u[...] += dot(x, wu[bx])
-        acc_r[...] += dot_nt(xg[1, bg].reshape(rows, fb), wd[:, pl.ds(pl.multiple_of(bg * fb, fb), fb)])
-        xt[bx] = x.T
-        for w in (wg, wu):
-            for k in range(hu // fb):
-                w[bx, :, k * fb : (k + 1) * fb] = w[bx, :, k * fb : (k + 1) * fb].T
-
-    loop(0, NH, gather_step)
+                gather_end(X_NEXT, *near)
+                gather_end(G_FAR, *near)
+                gather_end(X_FAR, *far)
+
+        hx, hg = [], []
+        for k in (2 * j, 2 * j + 1):
+            hx.append(blk(0, m4(cx + pick(k, o_of)), m4(cy + pick(k, q_of))))
+            hg.append(raw_block(k))
+
+        for k in range(2):
+            five = xg.at[1, hg[k], pl.ds(1, 5)]
+            to_tok(five, five, zs.at[2], zg.at[2 * j + k], partner(0, True)).wait_recv()
+        pair(hx, hg)
+
+    def pair(hx, hg):
+        x = jnp.concatenate([xg[0, h].reshape(rows, fb) for h in hx], axis=1)
+        acc_g[...] += dot(x, jnp.concatenate([wg[h] for h in hx], axis=0))
+        acc_u[...] += dot(x, jnp.concatenate([wu[h] for h in hx], axis=0))
+        acc_r[...] += dot_nt(
+            jnp.concatenate([xg[1, h].reshape(rows, fb) for h in hg], axis=1),
+            jnp.concatenate([wd[:, pl.ds(pl.multiple_of(h * fb, fb), fb)] for h in hg], axis=1))
+        for h in hx:
+            xt[h] = xg[0, h].reshape(rows, fb).T
+            for w in (wg, wu):
+                for k in range(hu // fb):
+                    w[h, :, k * fb : (k + 1) * fb] = w[h, :, k * fb : (k + 1) * fb].T
+
+    p_recv().wait_recv()
+    loop(0, NH // 2, gather_step)
 
     def deltas(b):
         at = pl.ds(pl.multiple_of(b * cap, cap), cap)
@@ -492,9 +520,14 @@
     near = partner(0, False)
     beside = along(0, 0)
     ends = [
-        to_tok(pack.at[:, pl.ds(0, n_z)], pack.at[:, pl.ds(0, n_z)], zs.at[0], zr.at[0, 0], near),
+        to_tok(pack.at[pl.ds(0, n_z)], pack.at[pl.ds(0, n_z)], zs.at[0], zr.at[0, 0], near),
+        to_tok(xg.at[0, pl.ds(0, 10)], xg.at[0, pl.ds(0, 10)], zs.at[2], zr.at[0, 0], near),
+        to_tok(pk.at[0, pl.ds(0, 2)], pk.at[0, pl.ds(0, 2)], zs.at[3], zr.at[0, 0], near),
         to_tok(psend.at[pl.ds(0, n_z)], psend.at[pl.ds(0, n_z)], zs.at[1], zr.at[0, 0], near),
-        to_hid(xg.at[:, pl.ds(0, NH - 1)], xg.at[:, pl.ds(0, NH - 1)], gs.at[0], gf.at[0, 0], beside),
+        to_hid(xg.at[0, pl.ds(0, NH - 1)], xg.at[0, pl.ds(0, NH - 1)], gs.at[0], gf.at[0, 0], beside),
+        to_hid(xg.at[1, pl.ds(0, NH - 1), pl.ds(6, 2)], xg.at[1, pl.ds(0, NH - 1), pl.ds(6, 2)],
+               gs.at[1], gf.at[0, 0], beside),
+        to_hid(raw.at[pl.ds(0, NH - 1)], raw.at[pl.ds(0, NH - 1)], gs.at[2], gf.at[0, 0], beside),
         to_hid(rl1s, rl1r, r1s.at[0], gf.at[0, 0], beside),
         to_hid(fn1s, fn1s, r1s.at[1], gf.at[0, 0], beside),
         to_hid(rl2s, rl2r, r1s.at[2], gf.at[0, 0], beside),
@@ -543,10 +576,10 @@
         in_specs=[hbm_spec] * 7,
         out_specs=(vm_spec,) * 5,
         scratch_shapes=[
-            vmem((2, n_tok), I32), vmem((2, n_tok), BF), vmem((n_tok, fb), BF), vmem((n_tok, fb), BF),
+            vmem((2, n_tok), I32), vmem((2, n_tok), BF), vmem((n_tok, fb), BF), vmem((NH, n_tok, fb), BF),
             vmem((NH, fb, hu), BF), vmem((NH, fb, hu), BF), vmem((hu, width), BF),
-            vmem((NT, cap, n_tok), F32), vmem((n_tok, rows), F32),
-            vmem((2, NT, cap, fb), BF), vmem((NT, 8, n_tok), F32), vmem((NT, 8, n_tok), F32),
+            vmem((NT, cap, n_tok), F32), vmem((rows, n_tok), BF), vmem((n_tok, rows), F32),
+            vmem((NT, cap, fb), BF), vmem((NH, NT, cap, fb), BF), vmem((NT, 8, n_tok), F32), vmem((NT, 8, n_tok), F32),
             vmem((2, NH, NT, cap, fb), BF), vmem((NH, fb, rows), BF),
             vmem((rows, hu), F32), vmem((rows, hu), F32), vmem((rows, hu), F32),
             vmem((rows, 2 * hu), BF), vmem((rows, hu), BF), vmem((hu, rows), BF),
@@ -559,13 +592,13 @@
             vmem((2, 2, 2, hr // 2, fb), BF), vmem((2, 2, 2, hr // 2, fb), BF),
             vmem((NT, cap, fb), BF), vmem((NT, cap, fb), BF),
             dma((7,)),
-            dma((2,)), dma((3, 3)),
-            dma((1,)), dma((3, 2, 11)), dma((2, 4)),
+            dma((4,)), dma((3, 3)), dma((NH,)),
+            dma((3,)), dma((5, 11)), dma((5, 4)),
             dma((4,)), dma((2, 2, 2)), dma((2, 4)), dma((2, 2)), dma((2,)),
             dma((2,)), dma((2,)), dma((2,)), dma((2,)),
         ],
         compiler_params=pltpu.CompilerParams(
-            collective_id=0, has_side_effects=True, vmem_limit_bytes=46 * 1024 * 1024
+            collective_id=0, has_side_effects=True, vmem_limit_bytes=50 * 1024 * 1024
         ),
     )(*[
         pltpu.with_memory_space_constraint(a, pltpu.HBM)

time: 77.1 us -> 73 us (0.947)
  Pallas kernels: 76.3 us -> 72.2 us
    pallas_call x1, Pallas kernels: 71.6 us -> 67.5 us  [per_device(): pl.pallas_call(exchange, name='exchange', out_shape=tuple((vmem(s.shape,...]
where the time goes in v5:
time: 73 us; the launch traced here: 72.9 us
  Pallas kernels  72.2 us (99%)
    pallas_call x1, Pallas kernels, per_device(): pl.pallas_call(exchange, name='exchange', out_shape=tuple((vmem(s.shape,...  67.5 us
    pallas_call x1, Pallas kernels, per_device(): pl.pallas_call(copy_out, name='copy_out', out_shape=shapes, in_specs=[vm_...  4.73 us

profile of v5, /device:TPU:1, one launch (start us, length us, event | category | flops | bytes accessed | tf_op | source)
XLA Modules:
  0.0 72.9 jit_solution(7715602803294695571)
XLA Ops:
  0.6 67.5 %exchange.1 = (bf16[128,256]{1,0:T(8,128)(2,1)S(1)}, bf16[2,128]{1,0:T(2,128)(2,1)S(1)}, bf16[4096,512]{1,0:T(8,128)(2,1)S(1)}, bf16[4096,512]{1,0:T(8,128)(2,1)S(1)}, bf16[512,4096]{1,0:T(8,128)(2,1)S(1)}) custom-call(s32[2,128]{1,0:T(2,128)} %bitcast.12, bf16[2,128]{1,0:T(2,128)(2,1)} %bitcast.13, bf16[128,256]{1,0:T(8,128)(2,1)} %tok_hbm.1, ...), custom_call_target="tpu_custom_call" | custom-call | tf_op jit(solution)/shard_map/exchange/pallas_call | solution.py:572
  68.2 4.7 %copy_out.1 = (bf16[128,256]{1,0:T(8,128)(2,1)}, bf16[2,128]{1,0:T(2,128)(2,1)}, bf16[4096,512]{1,0:T(8,128)(2,1)}, bf16[4096,512]{1,0:T(8,128)(2,1)}, bf16[512,4096]{1,0:T(8,128)(2,1)}) custom-call(bf16[128,256]{1,0:T(8,128)(2,1)S(1)} %get-tuple-element.15.refs_0_, bf16[2,128]{1,0:T(2,128)(2,1)S(1)} %get-tuple-element.16.refs_1_, ...), custom_call_target="tpu_custom_call" | custom-call | tf_op jit(solution)/shard_map/copy_out/pallas_call | solution.py:610

commit v6 on v5

--- a/solution.py
+++ b/solution.py
@@ -202,20 +202,33 @@
         g, p, s = frame(st)
         return gather_copy(st, blk(g, m4(p + o), m4(s - SIGN[d])), d, 11 + o, blk(g, p, m4(s + SIGN[d])))
 
-    def gather_begin(st):
-        for d in range(2):
-            p_own(st, d).start()
-            s_own(st, 0, d).start()
+    def gather_begin(*sts):
+        for st in sts:
+            for d in range(2):
+                p_own(st, d).start()
+        for st in sts:
+            for d in range(2):
+                s_own(st, 0, d).start()
+
+    def gather_p(*sts):
+        for st in sts:
+            for d in range(2):
+                p_own(st, d, True).wait_recv()
+                p_fwd(st, d).start()
+        for st in sts:
+            for d in range(2):
+                for d2 in range(2):
+                    s_own(st, (4 - SIGN[d]) % 4, d2).start()
+
+    def gather_s(*sts):
+        for st in sts:
+            for d in range(2):
+                s_own(st, 0, d, True).wait_recv()
+                s_fwd(st, 0, d).start()
 
     def gather_1(st):
-        for d in range(2):
-            p_own(st, d, True).wait_recv()
-            p_fwd(st, d).start()
-            for d2 in range(2):
-                s_own(st, (4 - SIGN[d]) % 4, d2).start()
-        for d in range(2):
-            s_own(st, 0, d, True).wait_recv()
-            s_fwd(st, 0, d).start()
+        gather_p(st)
+        gather_s(st)
 
     def gather_5(st):
         g, p, s = frame(st)
@@ -247,7 +260,7 @@
         for m in range(5):
             to = partner(m, False)
             place = 2 * PLACE[-PARTNERS[m][0] % 4] + core
-            to_tok(pk.at[h, to], xg.at[1, h, place], zs.at[2], zg.at[n], to).start()
+            to_tok(pk.at[h, to], xg.at[1, h, place], zs.at[2], zg.at[lax.div(n, 2)], to).start()
 
     def raw_packs(*places):
         loop(0, len(places), lambda i: raw_pack(pick(i, places)))
@@ -278,26 +291,27 @@
     gather_pass(X_OWN, 3, 1)
     gather_pass(RAW, 2)
     z_recv(0, 1).wait_recv()
-    gather_begin(X_NEXT)
     z_recv(0, 2).wait_recv()
-    gather_begin(X_FAR)
     z_recv(1, 2).wait_recv()
-    gather_begin(G_FAR)
+    gather_begin(X_FAR, G_FAR, X_NEXT)
     raw_packs(11, 13)
     gather_pass(X_OWN, 2)
+    gather_p(X_FAR, X_NEXT, G_FAR)
     gather_end(RAW, 0, 3, 1, 2)
     raw_packs(10, 12, 14, 15)
-    for st in (X_NEXT, X_FAR, G_FAR):
-        gather_1(st)
+    gather_s(X_FAR, X_NEXT, G_FAR)
     for c in w_copies:
         c.wait()
     gather_end(X_OWN, 0, 3, 1, 2)
 
     def gather_step(j):
+        @pl.when(j == 1)
+        def _():
+            for st in (X_FAR, X_NEXT, G_FAR):
+                gather_5(st)
+
         @pl.when(j == 2)
         def _():
-            for st in (X_NEXT, X_FAR, G_FAR):
-                gather_5(st)
             for st in (X_NEXT, X_FAR, G_FAR):
                 gather_pass(st, 3, 1)
 
@@ -318,9 +332,8 @@
             hx.append(blk(0, m4(cx + pick(k, o_of)), m4(cy + pick(k, q_of))))
             hg.append(raw_block(k))
 
-        for k in range(2):
-            five = xg.at[1, hg[k], pl.ds(1, 5)]
-            to_tok(five, five, zs.at[2], zg.at[2 * j + k], partner(0, True)).wait_recv()
+        ten = xg.at[1, pl.ds(0, 2), pl.ds(0, 5)]
+        to_tok(ten, ten, zs.at[2], zg.at[j], partner(0, True)).wait_recv()
         pair(hx, hg)
 
     def pair(hx, hg):
@@ -347,14 +360,19 @@
         p = jnp.sum(jnp.where(diag, precv[b, 0:1, :], 0.0), axis=1, keepdims=True)
         s = 1.0 / (1.0 + jnp.exp(-g))
         act = g * s
-        au = act * u
-        hp[at, :] = (au * p).astype(BF)
-        q = jnp.sum(au.astype(BF).astype(F32) * r, axis=1, keepdims=True)
-        qs[pl.ds(b, 1), :] = jnp.sum(jnp.where(diag, q, 0.0), axis=0, keepdims=True)
         rp = r * p
         dd[at, 0:hu] = (rp * u * s * (1.0 + g * (1.0 - s))).astype(BF)
         dd[at, hu : 2 * hu] = (rp * act).astype(BF)
 
+    def hiddens(b):
+        at = pl.ds(pl.multiple_of(b * cap, cap), cap)
+        g = acc_g[at, :]
+        p = jnp.sum(jnp.where(diag, precv[b, 0:1, :], 0.0), axis=1, keepdims=True)
+        au = g * (1.0 / (1.0 + jnp.exp(-g))) * acc_u[at, :]
+        hp[at, :] = (au * p).astype(BF)
+        q = jnp.sum(au.astype(BF).astype(F32) * acc_r[at, :], axis=1, keepdims=True)
+        qs[pl.ds(b, 1), :] = jnp.sum(jnp.where(diag, q, 0.0), axis=0, keepdims=True)
+
     loop(0, NT, deltas)
 
     hrows = rows // 2
@@ -368,7 +386,7 @@
         return blk(a, p, m4(s + SIGN[d]))
 
     def rl1(a, d, i):
-        return to_hid(rl1s.at[a, d, i], rl1r.at[a, d, i], r1s.at[0], r1r.at[a, d, i], along(a, d))
+        return to_hid(rl1s.at[a, d, i], rl1r.at[d, i, a], r1s.at[0], r1r.at[d, i], along(a, d))
 
     def fn1(a, d, q):
         return to_hid(fn1s.at[a, d, q], fn1r.at[a, q, d], r1s.at[1], f1r.at[a, q], along(a, d))
@@ -403,30 +421,28 @@
                     rl1s[a, d, i] = e32[where[k % 2], a].astype(BF)
                     rl1(a, d, i).start()
 
-    q1[cx] = qs[...]
-    for k in range(1, 4):
-        q_x(k).start()
-    loop(0, NH // 2, e_step)
-
     relayed = {2: (0, 0), 1: (0, 1), 3: (1, 0), 0: (1, 1)}
 
+    def first_send(q, d):
+        way, i = relayed[q]
+        if d == way:
+            to_hid(rl1r.at[d, i], rl1r.at[d, i], r1s.at[0], r1r.at[d, i], along(0, d)).wait_recv()
+        for a in range(2):
+            e = e32[blk(a, m4(prim[a] + SIGN[d]), m4(seco[a] + q)), a]
+            if d == way:
+                e = e + rl1r[d, i, a].astype(F32)
+            fn1s[a, d, q] = e.astype(BF)
+            fn1(a, d, q).start()
+
     def first_step(q):
-        way, i = relayed[q]
-        for d in (1 - way, way):
-            for a in range(2):
-                e = e32[blk(a, m4(prim[a] + SIGN[d]), m4(seco[a] + q)), a]
-                if d == way:
-                    rl1(a, d, i).wait_recv()
-                    e = e + rl1r[a, d, i].astype(F32)
-                fn1s[a, d, q] = e.astype(BF)
-                fn1(a, d, q).start()
+        way = relayed[q][0]
+        first_send(q, 1 - way)
+        first_send(q, way)
 
     def total_of(a, q):
         to_hid(fn1r.at[a, q], fn1r.at[a, q], r1s.at[1], f1r.at[a, q], along(a, 0)).wait_recv()
         return (e32[blk(a, prim[a], m4(seco[a] + q)), a]
                 + fn1r[a, q, 0].astype(F32) + fn1r[a, q, 1].astype(F32))
-
-    hpt[...] = hp[...].T
 
     def weight_step(c):
         at = pl.ds(pl.multiple_of(2 * c * fb, 2 * fb), 2 * fb)
@@ -438,16 +454,19 @@
             down_ref[:, pl.ds(pl.multiple_of(h * fb, fb), fb)] = dot(
                 hpt[...], xg[1, h].reshape(rows, fb)).astype(BF)
 
-    first_step(2)
-    first_step(3)
-    to_hid(q1.at[pl.ds(0, 3)], q1.at[pl.ds(0, 3)], qss.at[0], qsr.at[0], along(0, 0)).wait_recv()
-    qt[...] = q1[0] + q1[1] + q1[2] + q1[3]
-    q2[cy] = qt[...]
+    loop(0, 4, e_step)
+    first_send(2, 1)
+    loop(4, NH // 2, e_step)
+    first_send(3, 0)
+    first_send(2, 0)
+    first_send(3, 1)
+    loop(0, NT, hiddens)
+    q1[cx] = qs[...]
     for k in range(1, 4):
-        q_y(k).start()
+        q_x(k).start()
+    first_step(1)
+    hpt[...] = hp[...].T
     loop(0, 2, weight_step)
-    first_step(1)
-    loop(2, 3, weight_step)
     quarter = hrows // 2
     for a in range(2):
         s = total_of(a, 2)
@@ -455,20 +474,13 @@
             rl2s[a, d] = s[d * quarter : (d + 1) * quarter].astype(BF)
             rl2(a, d).start()
     first_step(0)
-    loop(3, 6, weight_step)
-    to_hid(q2.at[pl.ds(0, 3)], q2.at[pl.ds(0, 3)], qss.at[1], qsr.at[1], across(0, 0)).wait_recv()
-    qw = q2[0] + q2[1] + q2[2] + q2[3]
-    qsum = qb.at[NT]
-    qsum[...] = qw
-    qb[t] = qw
-
-    def c_send(m):
-        to = partner(m, False)
-        return to_tok(qb.at[NT], qb.at[t], bs.at[1], br.at[1], to)
-
-    for m in range(7):
-        c_send(m).start()
-
+    loop(2, 3, weight_step)
+    to_hid(q1.at[pl.ds(0, 3)], q1.at[pl.ds(0, 3)], qss.at[0], qsr.at[0], along(0, 0)).wait_recv()
+    qt[...] = q1[0] + q1[1] + q1[2] + q1[3]
+    q2[cy] = qt[...]
+    for k in range(1, 4):
+        q_y(k).start()
+    loop(3, 4, weight_step)
     for d, q in ((1, 3), (0, 1)):
         for a in range(2):
             s = total_of(a, q)
@@ -479,7 +491,20 @@
             fn2s[a, d, d] = (s[at] + r).astype(BF)
             fn2s[a, d, 1 - d] = s[other].astype(BF)
             fn2(a, d).start()
-    loop(6, 8, weight_step)
+    loop(4, 5, weight_step)
+    to_hid(q2.at[pl.ds(0, 3)], q2.at[pl.ds(0, 3)], qss.at[1], qsr.at[1], across(0, 0)).wait_recv()
+    qw = q2[0] + q2[1] + q2[2] + q2[3]
+    qsum = qb.at[NT]
+    qsum[...] = qw
+    qb[t] = qw
+
+    def c_send(m):
+        to = partner(m, False)
+        return to_tok(qb.at[NT], qb.at[t], bs.at[1], br.at[1], to)
+
+    for m in range(7):
+        c_send(m).start()
+
 
     def b_send(m):
         to = partner(m, False)
@@ -492,10 +517,11 @@
         for d in range(2):
             s = s + fn2r[a, d].astype(F32).reshape(hrows, fb)
         shr[a * half : (a + 1) * half] = s.astype(BF).reshape(half, cap, fb)
-        for m, (dz, dc) in enumerate(PARTNERS):
-            if PLACE[dz] // 2 == a:
+        for m in (5, 6, 0, 1, 2, 3, 4):
+            if PLACE[PARTNERS[m][0]] // 2 == a:
                 b_send(m).start()
     rb[t] = shr[core]
+    loop(5, 8, weight_step)
 
     def back_wait(ref, k):
         ref = ref.at[pl.ds(0, len(PARTNERS))]
@@ -592,9 +618,9 @@
             vmem((2, 2, 2, hr // 2, fb), BF), vmem((2, 2, 2, hr // 2, fb), BF),
             vmem((NT, cap, fb), BF), vmem((NT, cap, fb), BF),
             dma((7,)),
-            dma((4,)), dma((3, 3)), dma((NH,)),
+            dma((4,)), dma((3, 3)), dma((NH // 2,)),
             dma((3,)), dma((5, 11)), dma((5, 4)),
-            dma((4,)), dma((2, 2, 2)), dma((2, 4)), dma((2, 2)), dma((2,)),
+            dma((4,)), dma((2, 2)), dma((2, 4)), dma((2, 2)), dma((2,)),
             dma((2,)), dma((2,)), dma((2,)), dma((2,)),
         ],
         compiler_params=pltpu.CompilerParams(

time: 73 us -> 72.4 us (level)
  no operation moved by 1% of the time
where the time goes in v6:
time: 72.4 us; the launch traced here: 72.3 us
  Pallas kernels  71.6 us (99%)
    pallas_call x1, Pallas kernels, per_device(): pl.pallas_call(exchange, name='exchange', out_shape=tuple((vmem(s.shape,...  66.9 us
    pallas_call x1, Pallas kernels, per_device(): pl.pallas_call(copy_out, name='copy_out', out_shape=shapes, in_specs=[vm_...  4.73 us

profile of v6, /device:TPU:1, one launch (start us, length us, event | category | flops | bytes accessed | tf_op | source)
XLA Modules:
  0.0 72.3 jit_solution(10795241068645095700)
XLA Ops:
  0.6 66.9 %exchange.1 = (bf16[128,256]{1,0:T(8,128)(2,1)S(1)}, bf16[2,128]{1,0:T(2,128)(2,1)S(1)}, bf16[4096,512]{1,0:T(8,128)(2,1)S(1)}, bf16[4096,512]{1,0:T(8,128)(2,1)S(1)}, bf16[512,4096]{1,0:T(8,128)(2,1)S(1)}) custom-call(s32[2,128]{1,0:T(2,128)} %bitcast.12, bf16[2,128]{1,0:T(2,128)(2,1)} %bitcast.13, bf16[128,256]{1,0:T(8,128)(2,1)} %tok_hbm.1, ...), custom_call_target="tpu_custom_call" | custom-call | tf_op jit(solution)/shard_map/exchange/pallas_call | solution.py:598
  67.5 4.7 %copy_out.1 = (bf16[128,256]{1,0:T(8,128)(2,1)}, bf16[2,128]{1,0:T(2,128)(2,1)}, bf16[4096,512]{1,0:T(8,128)(2,1)}, bf16[4096,512]{1,0:T(8,128)(2,1)}, bf16[512,4096]{1,0:T(8,128)(2,1)}) custom-call(bf16[128,256]{1,0:T(8,128)(2,1)S(1)} %get-tuple-element.15.refs_0_, bf16[2,128]{1,0:T(2,128)(2,1)S(1)} %get-tuple-element.16.refs_1_, ...), custom_call_target="tpu_custom_call" | custom-call | tf_op jit(solution)/shard_map/copy_out/pallas_call | solution.py:636

commit v7 on v6

--- a/solution.py
+++ b/solution.py
@@ -394,8 +394,8 @@
     def rl2(a, d):
         return to_hid(rl2s.at[a, d], rl2r.at[a, d], r1s.at[2], r2r.at[a, d], across(a, d))
 
-    def fn2(a, d):
-        return to_hid(fn2s.at[a, d], fn2r.at[a, d], r1s.at[3], f2r.at[a], across(a, d))
+    def fn2(a, d, k):
+        return to_hid(fn2s.at[a, d, k], fn2r.at[a, d, k], r1s.at[3], f2r.at[a], across(a, d))
 
     def q_x(k):
         return to_hid(qs, q1.at[cx], qss.at[0], qsr.at[0], 4 * m4(cx + k) + cy)
@@ -484,13 +484,16 @@
     for d, q in ((1, 3), (0, 1)):
         for a in range(2):
             s = total_of(a, q)
+            fn2s[a, d, 1 - d] = s[(1 - d) * quarter : (2 - d) * quarter].astype(BF)
+            fn2(a, d, 1 - d).start()
+    for d, q in ((1, 3), (0, 1)):
+        for a in range(2):
+            at = slice(d * quarter, (d + 1) * quarter)
+            s = e32[blk(a, prim[a], m4(seco[a] + q)), a, at]
+            s = s + fn1r[a, q, 0, at].astype(F32) + fn1r[a, q, 1, at].astype(F32)
             rl2(a, d).wait_recv()
-            r = rl2r[a, d].astype(F32)
-            at = slice(d * quarter, (d + 1) * quarter)
-            other = slice((1 - d) * quarter, (2 - d) * quarter)
-            fn2s[a, d, d] = (s[at] + r).astype(BF)
-            fn2s[a, d, 1 - d] = s[other].astype(BF)
-            fn2(a, d).start()
+            fn2s[a, d, d] = (s + rl2r[a, d].astype(F32)).astype(BF)
+            fn2(a, d, d).start()
     loop(4, 5, weight_step)
     to_hid(q2.at[pl.ds(0, 3)], q2.at[pl.ds(0, 3)], qss.at[1], qsr.at[1], across(0, 0)).wait_recv()
     qw = q2[0] + q2[1] + q2[2] + q2[3]

time: 72.4 us -> 71.8 us (level)
  no operation moved by 1% of the time
where the time goes in v7:
time: 71.8 us; the launch traced here: 71.7 us
  Pallas kernels  71 us (99%)
    pallas_call x1, Pallas kernels, per_device(): pl.pallas_call(exchange, name='exchange', out_shape=tuple((vmem(s.shape,...  66.3 us
    pallas_call x1, Pallas kernels, per_device(): pl.pallas_call(copy_out, name='copy_out', out_shape=shapes, in_specs=[vm_...  4.73 us

profile of v7, /device:TPU:1, one launch (start us, length us, event | category | flops | bytes accessed | tf_op | source)
XLA Modules:
  0.0 71.7 jit_solution(14032898564356628950)
XLA Ops:
  0.6 66.3 %exchange.1 = (bf16[128,256]{1,0:T(8,128)(2,1)S(1)}, bf16[2,128]{1,0:T(2,128)(2,1)S(1)}, bf16[4096,512]{1,0:T(8,128)(2,1)S(1)}, bf16[4096,512]{1,0:T(8,128)(2,1)S(1)}, bf16[512,4096]{1,0:T(8,128)(2,1)S(1)}) custom-call(s32[2,128]{1,0:T(2,128)} %bitcast.12, bf16[2,128]{1,0:T(2,128)(2,1)} %bitcast.13, bf16[128,256]{1,0:T(8,128)(2,1)} %tok_hbm.1, ...), custom_call_target="tpu_custom_call" | custom-call | tf_op jit(solution)/shard_map/exchange/pallas_call | solution.py:601
  67.0 4.7 %copy_out.1 = (bf16[128,256]{1,0:T(8,128)(2,1)}, bf16[2,128]{1,0:T(2,128)(2,1)}, bf16[4096,512]{1,0:T(8,128)(2,1)}, bf16[4096,512]{1,0:T(8,128)(2,1)}, bf16[512,4096]{1,0:T(8,128)(2,1)}) custom-call(bf16[128,256]{1,0:T(8,128)(2,1)S(1)} %get-tuple-element.15.refs_0_, bf16[2,128]{1,0:T(2,128)(2,1)S(1)} %get-tuple-element.16.refs_1_, ...), custom_call_target="tpu_custom_call" | custom-call | tf_op jit(solution)/shard_map/copy_out/pallas_call | solution.py:639
